TPU v7x, 32 devices: a whole 2x2x4 slice. The times are simulated.
32 devices in a mesh: gx: 2 (over core), gy: 4 (over y, x), gz: 4 (over z).
Axes of the slice: x: 2, y: 2, z: 4, core: 2. Of those that a mesh axis runs over, the one named last changes fastest.
Arguments:
- displacement: float32 [3, 12, 24, 1536], P(None, 'gx', 'gy', 'gz'), may hold values from -0.18 to 0.18
- size_field_modes: float32 [27, 4, 8, 512], P(None, 'gx', 'gy', 'gz'), may hold values from -6 to 6
- velocity: float32 [3, 4, 8, 512], P(None, 'gx', 'gy', 'gz'), may hold values from -1 to 1
Outputs:
- advected_field: float32 [27, 4, 8, 512], P(None, 'gx', 'gy', 'gz')
- gradient: float32 [3, 12, 24, 1536], P(None, 'gx', 'gy', 'gz')
- checks: float32 [3], replicated
All inputs are finite; a program needn't handle non-finite values. Where the computation divides by a largest or mean magnitude, that divisor is 1e-20 or more.
Results may differ from a plain program's by a relative error of at most 0.0001.
Values sent between devices are 32-bit elements; how exact they have to be, the bound alone decides.
A program may use at most 64 MiB of HBM per device.

v0:
```python
import functools

import jax
import jax.numpy as jnp
import numpy as np
from jax import lax
from jax.experimental import pallas as pl
from jax.experimental.pallas import tpu as pltpu
from jax.sharding import PartitionSpec as P

SUBSTEPS = 4
MESH = pl.DeviceIdType.MESH
AXES = ("gx", "gy", "gz")

plus_values = (0.7071067811865476, 1.224744871391589, 1.5811388300841898)
g10 = 1.7320508075688772
g21 = 3.872983346207417
courant = 0.1
theta_size = 0.3
trial_step = 0.05


def tables_1d():
    points = np.array(
        [-0.8611363115940526, -0.3399810435848563, 0.3399810435848563, 0.8611363115940526]
    )
    weights = np.array(
        [0.3478548451374538, 0.6521451548625461, 0.6521451548625461, 0.3478548451374538]
    )
    points = 0.5 * (points + 1.0)
    weights = 0.5 * weights
    nodes = np.array([0.0, 1.0 / 3.0, 2.0 / 3.0, 1.0])
    value = np.zeros((4, 4))
    slope = np.zeros((4, 4))
    for m in range(4):
        others = [nodes[o] for o in range(4) if o != m]
        den = np.prod([nodes[m] - o for o in others])
        for q in range(4):
            g = points[q]
            value[q, m] = np.prod([g - o for o in others]) / den
            slope[q, m] = (
                sum(np.prod([g - others[t] for t in range(3) if t != s]) for s in range(3)) / den
            )
    c = 2.0 * points - 1.0
    legendre = np.stack(
        [
            np.full(4, plus_values[0]),
            plus_values[1] * c,
            plus_values[2] * 0.5 * (3.0 * c**2 - 1.0),
        ],
        axis=1,
    )
    return value, slope, legendre, weights


def row_tables(Y, Z):
    value, slope, legendre, weights = tables_1d()
    rows, nodes = 4 * Y, 3 * Y + 1
    tv = np.zeros((rows, rows))
    td = np.zeros((rows, rows))
    for e in range(Y):
        tv[4 * e : 4 * e + 4, 3 * e : 3 * e + 4] = value
        td[4 * e : 4 * e + 4, 3 * e : 3 * e + 4] = slope
    blocks = [tv[:, j] for j in range(nodes)] + [td[:, j] for j in range(nodes)]
    blocks += [tv[s, :] for s in range(rows)] + [td[s, :] for s in range(rows)]
    for b in range(3):
        for e in range(Y):
            col = np.zeros(rows)
            col[4 * e : 4 * e + 4] = legendre[:, b]
            blocks.append(col)
    blocks.append(np.tile(weights, Y))
    stacked = np.stack(blocks).astype(np.float32)
    return np.ascontiguousarray(np.broadcast_to(stacked[:, :, None], stacked.shape + (Z,)))


def kernel(sizes, X, Y, Z, disp, modes, vel, tab, adv, grad, checks,
           perm, slab, U, W, VEL, FS, SX, RX, SY, RY, SZ, RZ,
           RED, REDR, N, GN, A, G, J, B, SIZ, DT,
           NXR, NYS, NYR, NZS, NZR, FXR, FYS, FYR, FZS, FZR,
           hs, hr, rs, rr, ns, nr, fs, fr):
    value, slope, legendre, weights = tables_1d()
    NX, NY = 3 * X, 3 * Y
    ROWS = 4 * Y
    EL = X * Y
    f32 = jnp.float32
    index = [lax.axis_index(a) for a in AXES]
    lane = lax.broadcasted_iota(jnp.int32, (ROWS, Z), 1)
    row = lax.broadcasted_iota(jnp.int32, (ROWS, Z), 0)
    oTV, oTD, oGV, oGD, oL, oW = 0, NY + 1, 2 * NY + 2, 2 * NY + 2 + ROWS, 2 * NY + 2 + 2 * ROWS, 2 * NY + 2 + 2 * ROWS + 3 * Y

    def at(axis, by):
        n = sizes[axis]
        return {AXES[axis]: lax.rem(index[axis] + (by + n), n)}

    barrier = pltpu.get_barrier_semaphore()
    total = 0
    moves = [(by, 0, 0) for by in range(1, sizes[0])]
    moves += [(0, b, c) for b in range(sizes[1]) for c in range(sizes[2]) if b or c]
    for move in moves:
        target = {}
        for axis in range(3):
            if move[axis]:
                target.update(at(axis, move[axis]))
        pl.semaphore_signal(barrier, inc=1, device_id=target, device_id_type=MESH)
        total += 1

    def copy(src, dst, ss, sr, axis, by):
        return pltpu.make_async_remote_copy(
            src_ref=src, dst_ref=dst, send_sem=ss, recv_sem=sr,
            device_id=at(axis, by), device_id_type=MESH,
        )

    U[...] = jnp.zeros_like(U)
    VEL[...] = jnp.zeros_like(VEL)
    for ix in range(X):
        U[:, ix * Y : ix * Y + Y, :] = modes[:, ix]
        VEL[:, ix * Y : ix * Y + Y, :] = vel[:, ix]
    RED[0, 0] = jnp.zeros_like(RED[0, 0])
    RED[0, 0, 0] = jnp.abs(VEL[0]) + jnp.abs(VEL[1]) + jnp.abs(VEL[2])
    def unweave():
        a_i = lax.broadcasted_iota(jnp.int32, (3 * Z, 3 * Z), 0)
        b_i = lax.broadcasted_iota(jnp.int32, (3 * Z, 3 * Z), 1)
        b_k = (b_i >= Z).astype(jnp.int32) + (b_i >= 2 * Z).astype(jnp.int32)
        perm[...] = (a_i == 3 * (b_i - b_k * Z) + b_k).astype(f32)
        slab[...] = jnp.zeros_like(slab)
        for c in range(3):
            for i in range(NX):
                slab[c * NX + i, 0:NY, :] = disp[c, i]
        spread = jnp.dot(
            slab[...].reshape(3 * NX * ROWS, 3 * Z), perm[...],
            precision=lax.Precision.HIGHEST, preferred_element_type=f32,
        ).reshape(3, NX, ROWS, 3 * Z)
        for c in range(3):
            for k in range(3):
                N[c, 0:NX, k] = spread[c, :, :, k * Z : (k + 1) * Z]

    pl.semaphore_wait(barrier, total)

    def peers_of(phase):
        if phase == 0:
            return [(by, 0, 0) for by in range(1, sizes[0])]
        return [(0, b, c) for b in range(sizes[1]) for c in range(sizes[2]) if b or c]

    def red_copies(r, phase):
        off = 0 if phase == 0 else sizes[0] - 1
        out = []
        for n, move in enumerate(peers_of(phase)):
            target = {}
            for axis in range(3):
                if move[axis]:
                    target.update(at(axis, move[axis]))
            out.append(pltpu.make_async_remote_copy(
                src_ref=RED.at[r, phase], dst_ref=REDR.at[r, off + n],
                send_sem=rs.at[r, off + n], recv_sem=rr.at[r, off + n],
                device_id=target, device_id_type=MESH,
            ))
        return out

    def red_start(r, phase):
        for cp in red_copies(r, phase):
            cp.start()

    def red_finish(r, phase, op):
        off = 0 if phase == 0 else sizes[0] - 1
        copies = red_copies(r, phase)
        for cp in copies:
            cp.wait_recv()
        total = RED[r, phase]
        for n in range(len(copies)):
            total = op(total, REDR[r, off + n])
        RED[r, phase + 1] = total

    def rim_x(a, t):
        return copy(a.at[:, 0, 0:3], NXR.at[t], ns.at[t, 0], nr.at[t, 0], 0, -1)

    def rim_y(t):
        return copy(NYS.at[t], NYR.at[t], ns.at[t, 1], nr.at[t, 1], 1, -1)

    def rim_y_pack(a, t):
        for c in range(3):
            for k in range(3):
                a[c, NX, k] = NXR[t, c, k]
        for c in range(3):
            for i in range(NX + 1):
                for k in range(3):
                    NYS[t, c, i, k : k + 1, :] = a[c, i, k, 0:1, :]

    def rim_y_unpack(a, t):
        for c in range(3):
            for i in range(NX + 1):
                for k in range(3):
                    a[c, i, k, NY : NY + 1, :] = NYR[t, c, i, k : k + 1, :]

    def rim_z(t):
        return copy(NZS.at[t], NZR.at[t], ns.at[t, 2], nr.at[t, 2], 2, -1)

    def rim_z_pack(a, t):
        packed = jnp.zeros((ROWS, Z), f32)
        for c in range(3):
            for i in range(NX + 1):
                packed = jnp.where(lane == c * (NX + 1) + i, a[c, i, 0][:, 0:1], packed)
        NZS[t] = packed

    def rim_z_unpack(a, t):
        packed = NZR[t]
        for c in range(3):
            for i in range(NX + 1):
                at_ = c * (NX + 1) + i
                a[c, i, 3] = jnp.where(lane == Z - 1, packed[:, at_ : at_ + 1], pltpu.roll(a[c, i, 0], Z - 1, 1))

    def halo_copies(s, dims):
        out = []
        for d, (sb, rb) in ((0, (SX, RX)), (1, (SY, RY)), (2, (SZ, RZ))):
            if d not in dims:
                continue
            for way in range(2):
                out.append(copy(sb.at[s, way], rb.at[s, way], hs.at[s, 2 * d + way], hr.at[s, 2 * d + way], d, 1 - 2 * way))
        return out

    def send_part(s, n, d, tp, tm):
        if d == 0:
            SX[s, 0, n] = tp[(X - 1) * Y : EL]
            SX[s, 1, n] = tm[0:Y]
        else:
            for ix in range(X):
                SY[s, 0, n, ix : ix + 1] = tp[ix * Y + Y - 1 : ix * Y + Y]
                SY[s, 1, n, ix : ix + 1] = tm[ix * Y : ix * Y + 1]

    def prev_of(d, t, s, n):
        if d == 0:
            return jnp.concatenate([RX[s, 0, n], t[: ROWS - Y]], axis=0)
        if d == 1:
            parts = []
            for ix in range(X):
                parts += [RY[s, 0, n, ix : ix + 1], t[ix * Y : ix * Y + Y - 1]]
            return jnp.concatenate(parts + [t[EL:]], axis=0)
        return jnp.where(lane == 0, RZ[s, 0][:, n : n + 1], pltpu.roll(t, 1, 1))

    def next_of(d, t, s, n):
        if d == 0:
            return jnp.concatenate([t[Y:EL], RX[s, 1, n], t[EL:]], axis=0)
        if d == 1:
            parts = []
            for ix in range(X):
                parts += [t[ix * Y + 1 : ix * Y + Y], RY[s, 1, n, ix : ix + 1]]
            return jnp.concatenate(parts + [t[EL:]], axis=0)
        return jnp.where(lane == Z - 1, RZ[s, 1][:, n : n + 1], pltpu.roll(t, Z - 1, 1))

    strides = (9, 3, 1)
    others = [[m for m in range(27) if (m // strides[d]) % 3 == 0] for d in range(3)]

    def rate(src, s, first, between):
        u = [src[m] for m in range(27)]
        v = [VEL[d] for d in range(3)]
        tp, tm = [[], [], []], [[], [], []]
        for d in (2, 1, 0):
            for m in others[d]:
                even = plus_values[0] * u[m] + plus_values[2] * u[m + 2 * strides[d]]
                odd = plus_values[1] * u[m + strides[d]]
                tp[d].append(even + odd)
                tm[d].append(even - odd)
            ups = tp[d] + [v[d]]
            lows = tm[d] + [v[d]]
            if d == 2:
                up, low = jnp.zeros((ROWS, Z), f32), jnp.zeros((ROWS, Z), f32)
                for n in range(10 if first else 9):
                    up = jnp.where(lane == n, ups[n][:, Z - 1 : Z], up)
                    low = jnp.where(lane == n, lows[n][:, 0:1], low)
                SZ[s, 0] = up
                SZ[s, 1] = low
            else:
                for n in range(10):
                    send_part(s, n, d, ups[n], lows[n])
            for cp in halo_copies(s, (d,)):
                cp.start()
        acc = [None] * 27
        for d in range(3):
            st = strides[d]
            va, vb = (2.0 * g10) * v[d], (2.0 * g21) * v[d]
            for m in others[d]:
                for mm, term in ((m + st, va * u[m]), (m + 2 * st, vb * u[m + st])):
                    acc[mm] = term if acc[mm] is None else acc[mm] + term
        between()
        for d in range(3):
            for cp in halo_copies(s, (d,)):
                cp.wait_recv()
            if first:
                high = v[d] + next_of(d, v[d], s, 9)
                lowf = prev_of(d, v[d], s, 9) + v[d]
                FS[d, 0] = jnp.maximum(high, 0.0)
                FS[d, 1] = jnp.minimum(high, 0.0)
                FS[d, 2] = jnp.maximum(lowf, 0.0)
                FS[d, 3] = jnp.minimum(lowf, 0.0)
            st = strides[d]
            hp, hm, lp, lm = [FS[d, t] for t in range(4)]
            for n, m in enumerate(others[d]):
                hi = hp * tp[d][n] + hm * next_of(d, tm[d][n], s, n)
                lo = lp * prev_of(d, tp[d][n], s, n) + lm * tm[d][n]
                diff, both = lo - hi, lo + hi
                for mm, term in (
                    (m, plus_values[0] * diff),
                    (m + st, (-plus_values[1]) * both),
                    (m + 2 * st, plus_values[2] * diff),
                ):
                    acc[mm] = term if acc[mm] is None else acc[mm] + term
        return acc

    def yz_of(src):
        def yz(i, carry):
            for c in range(3):
                yv, yd = [], []
                for k in range(4):
                    sv = sd = None
                    for j in range(NY + 1):
                        x = src[c, i, k, j : j + 1, :]
                        tv, td = tab[oTV + j] * x, tab[oTD + j] * x
                        sv = tv if sv is None else sv + tv
                        sd = td if sd is None else sd + td
                    yv.append(sv)
                    yd.append(sd)
                for r in range(4):
                    A[0, c, i, r] = sum(float(value[r, k]) * yv[k] for k in range(4))
                    A[1, c, i, r] = sum(float(value[r, k]) * yd[k] for k in range(4))
                    A[2, c, i, r] = sum(float(slope[r, k]) * yv[k] for k in range(4))
            return carry

        lax.fori_loop(0, NX + 1, yz, 0)

    def slope_at(ix, p, r, c, d):
        tb = slope if d == 0 else value
        return sum(float(tb[p, m]) * A[d, c, 3 * ix + m, r] for m in range(4))

    def jacobians(t):
        ix, r = t // 4, t % 4
        for p in range(4):
            for c in range(3):
                for d in range(3):
                    jac = slope_at(ix, p, r, c, d)
                    J[d, c, ix, p, r] = jac + 1.0 if c == d else jac

    red_start(0, 0)

    def between_0():
        red_finish(0, 0, jnp.maximum)
        red_start(0, 1)
        unweave()
        rim_x(N, 0).start()

    def between_1():
        rim_x(N, 0).wait()
        rim_y_pack(N, 0)
        rim_y(0).start()
        red_finish(0, 1, jnp.maximum)

    def between_2():
        rim_y(0).wait()
        rim_y_unpack(N, 0)
        rim_z_pack(N, 0)
        rim_z(0).start()

    def between_3():
        rim_z(0).wait()
        rim_z_unpack(N, 0)
        yz_of(N)

    def two_stages(s, first, between_a, between_b, dt_of):
        w = rate(U, s, first, between_a)
        for m in range(27):
            W[m] = w[m]
        w = rate(W, s + 1, False, between_b)
        dt = dt_of()
        half = 0.5 * dt * dt
        for m in range(27):
            U[m] = U[m] + dt * W[m] + half * w[m]

    def time_step():
        fastest = jnp.max(RED[0, 2, 0], axis=(0, 1), keepdims=True)
        DT[...] = jnp.broadcast_to(courant / jnp.maximum(fastest, 0.25), (ROWS, Z))
        return DT[...]

    two_stages(0, True, between_0, between_1, time_step)
    two_stages(2, False, between_2, between_3, lambda: DT[...])
    units = (4 * X) // (2 * SUBSTEPS - 4)

    def substep(t, carry):
        def some(s):
            def run():
                for n in range(units):
                    jacobians((s - 4) * units + n)
            return run

        two_stages(2 * t, False, some(2 * t), some(2 * t + 1), lambda: DT[...])
        return carry

    lax.fori_loop(2, SUBSTEPS, substep, 0)
    def size_of(ix, carry):
        mid = {}
        for a in range(3):
            for r in range(4):
                mid[a, r] = None
            for c in range(3):
                t = None
                for b in range(3):
                    for e in range(Y):
                        term = tab[oL + b * Y + e] * U[a * 9 + b * 3 + c, pl.ds(ix * Y + e, 1), :]
                        t = term if t is None else t + term
                for r in range(4):
                    term = float(legendre[r, c]) * t
                    mid[a, r] = term if mid[a, r] is None else mid[a, r] + term
        for p in range(4):
            for r in range(4):
                s = sum(float(legendre[p, a]) * mid[a, r] for a in range(3))
                SIZ[ix, p, r] = jnp.exp(theta_size * s)
        return carry

    lax.fori_loop(0, X, size_of, 0)

    wrow = tab[oW]
    pairs = [(d, e) for d in range(3) for e in range(d, 3)]

    def dot3(p, q, d, e):
        return p[0][d] * q[0][e] + p[1][d] * q[1][e] + p[2][d] * q[2][e]

    def gauss_weight(r):
        return jnp.where((r == 0) | (r == 3), float(weights[0]), float(weights[1]))

    def gauss(t, esum):
        ix, r = t // 4, t % 4
        for p in range(4):
            size = SIZ[ix, p, r]
            inv = 1.0 / size
            M = [[J[d, c, ix, p, r] * inv for d in range(3)] for c in range(3)]
            D = [[None] * 3 for _ in range(3)]
            metric = None
            for d, e in pairs:
                dev = dot3(M, M, d, e)
                if d == e:
                    dev = dev - 1.0
                D[d][e] = D[e][d] = dev
                sq = dev * dev if d == e else 2.0 * (dev * dev)
                metric = sq if metric is None else metric + sq
            w = wrow * (gauss_weight(r) * float(weights[p]))
            size2 = size * size
            esum = esum + w * (size2 * size) * metric
            scale = (4.0 * w) * size2
            for c in range(3):
                for d in range(3):
                    g = M[c][0] * D[0][d] + M[c][1] * D[1][d] + M[c][2] * D[2][d]
                    G[d, c, ix, p, r] = scale * g
        return esum

    zero = jnp.zeros((ROWS, Z), f32)
    esum = lax.fori_loop(0, 4 * X, gauss, zero)

    def back_c(c, carry):
        for i in range(NX + 1):
            bv = [None] * 4
            bd = [None] * 4
            for r in range(4):
                ga = []
                for d in range(3):
                    tb = slope if d == 0 else value
                    acc = None
                    for ix in range(X):
                        m = i - 3 * ix
                        if 0 <= m <= 3:
                            for p in range(4):
                                term = float(tb[p, m]) * G[d, c, ix, p, r]
                                acc = term if acc is None else acc + term
                    ga.append(acc)
                for k in range(4):
                    tv = float(value[r, k]) * ga[0] + float(slope[r, k]) * ga[2]
                    td = float(value[r, k]) * ga[1]
                    bv[k] = tv if bv[k] is None else bv[k] + tv
                    bd[k] = td if bd[k] is None else bd[k] + td
            for k in range(4):
                B[0, i, k] = bv[k]
                B[1, i, k] = bd[k]
        for i in range(NX + 1):
            for k in range(4):
                acc = None
                for s in range(ROWS):
                    term = tab[oGV + s] * B[0, i, k, s : s + 1, :] + tab[oGD + s] * B[1, i, k, s : s + 1, :]
                    acc = term if acc is None else acc + term
                GN[c, i, k] = acc
        return carry

    lax.fori_loop(0, 3, back_c, 0)

    def both_ways(src_up, src_down, axis, slot, up, down):
        copies = [
            copy(src_up, up, fs.at[slot], fr.at[slot], axis, 1),
            copy(src_down, down, fs.at[slot + 1], fr.at[slot + 1], axis, -1),
        ]
        for cp in copies:
            cp.start()
        for cp in copies:
            cp.wait()

    up, down = zero, zero
    for c in range(3):
        for i in range(NX + 1):
            here = lane == c * (NX + 1) + i
            up = jnp.where(here, GN[c, i, 3][:, Z - 1 : Z], up)
            down = jnp.where(here, GN[c, i, 0][:, 0:1], down)
    FZS[0] = up
    FZS[1] = down
    both_ways(FZS.at[0], FZS.at[1], 2, 0, FZR.at[0], FZR.at[1])
    up, down = FZR[0], FZR[1]
    for c in range(3):
        for i in range(NX + 1):
            n = c * (NX + 1) + i
            g0, g3 = GN[c, i, 0], GN[c, i, 3]
            full = g0 + jnp.where(lane == 0, up[:, n : n + 1], pltpu.roll(g3, 1, 1))
            GN[c, i, 0] = full
            GN[c, i, 3] = jnp.where(lane == Z - 1, g3 + down[:, n : n + 1], pltpu.roll(full, Z - 1, 1))
    both_ways(GN.at[:, NX], GN.at[:, 0], 0, 2, FXR.at[0], FXR.at[1])
    for c in range(3):
        for k in range(4):
            GN[c, 0, k] = GN[c, 0, k] + FXR[0, c, k]
            GN[c, NX, k] = GN[c, NX, k] + FXR[1, c, k]
    for c in range(3):
        for i in range(NX + 1):
            for k in range(4):
                FYS[0, c, i, k : k + 1, :] = GN[c, i, k, NY : NY + 1, :]
                FYS[1, c, i, k : k + 1, :] = GN[c, i, k, 0:1, :]
    both_ways(FYS.at[0], FYS.at[1], 1, 4, FYR.at[0], FYR.at[1])
    for c in range(3):
        for i in range(NX + 1):
            for k in range(4):
                GN[c, i, k, 0:1, :] = GN[c, i, k, 0:1, :] + FYR[0, c, i, k : k + 1, :]
                GN[c, i, k, NY : NY + 1, :] = GN[c, i, k, NY : NY + 1, :] + FYR[1, c, i, k : k + 1, :]
    ssum = zero
    for c in range(3):
        for i in range(NX):
            for k in range(3):
                g = GN[c, i, k]
                ssum = ssum + g * g
    ssum = jnp.where(row < NY, ssum, 0.0)
    devices = sizes[0] * sizes[1] * sizes[2]
    elements = float(EL * Z * devices)
    entries = 81.0 * elements
    mine = jnp.sum(ssum, axis=(0, 1), keepdims=True)
    bound = trial_step / jnp.sqrt(1.0 + mine / entries)
    bound = jnp.broadcast_to(bound, (ROWS, Z))
    yz_of(GN)

    def trial(t, sums):
        ix, r = t // 4, t % 4
        s1, s2, s3, s4 = sums
        for p in range(4):
            size = SIZ[ix, p, r]
            inv = 1.0 / size
            move = -(inv * bound)
            M = [[J[d, c, ix, p, r] * inv for d in range(3)] for c in range(3)]
            K = [[slope_at(ix, p, r, c, d) * move for d in range(3)] for c in range(3)]
            w = wrow * (gauss_weight(r) * float(weights[p])) * (size * size * size)
            q = [None] * 4
            for d, e in pairs:
                d0 = dot3(M, M, d, e)
                d2 = dot3(K, K, d, e)
                if d == e:
                    d0 = d0 - 1.0
                    d1 = 2.0 * dot3(M, K, d, d)
                else:
                    d1 = dot3(M, K, d, e) + dot3(K, M, d, e)
                terms = [2.0 * (d0 * d1), d1 * d1 + 2.0 * (d0 * d2), 2.0 * (d1 * d2), d2 * d2]
                for n in range(4):
                    term = terms[n] if d == e else 2.0 * terms[n]
                    q[n] = term if q[n] is None else q[n] + term
            s1, s2, s3, s4 = s1 + w * q[0], s2 + w * q[1], s3 + w * q[2], s4 + w * q[3]
        return s1, s2, s3, s4

    sums = lax.fori_loop(0, 4 * X, trial, (zero,) * 4)
    block = zero
    for n, part in enumerate((esum, ssum) + tuple(sums)):
        block = jnp.where(row == n, jnp.sum(part, axis=0, keepdims=True), block)
    column = jnp.sum(block, axis=1, keepdims=True)
    column = jnp.where(row == 6, bound, jnp.broadcast_to(column, (ROWS, Z)))
    me = (index[0] * sizes[1] + index[1]) * sizes[2] + index[2]
    groups = RED.shape[2]
    for n in range(groups):
        RED[1, 0, n] = jnp.where(lane + n * Z == me, column, 0.0)
    red_start(1, 0)
    for c in range(3):
        for k in range(3):
            slab[c * NX : (c + 1) * NX, :, k * Z : (k + 1) * Z] = GN[c, 0:NX, k]
    red_finish(1, 0, jnp.add)
    red_start(1, 1)
    woven = lax.dot_general(
        slab[...].reshape(3 * NX * ROWS, 3 * Z), perm[...], (((1,), (1,)), ((), ())),
        precision=lax.Precision.HIGHEST, preferred_element_type=f32,
    ).reshape(3, NX, ROWS, 3 * Z)
    grad[...] = woven[:, :, 0:NY, :]
    for ix in range(X):
        adv[:, ix] = U[:, ix * Y : ix * Y + Y, :]
    red_finish(1, 1, jnp.add)
    every = [RED[1, 2, n] for n in range(groups)]

    def over_all(parts):
        return sum(jnp.sum(x, axis=1, keepdims=True) for x in parts)

    etot = over_all([x[0:1] for x in every])
    stot = over_all([x[1:2] for x in every])
    step = trial_step / jnp.sqrt(1.0 + stot / entries)
    parts = []
    for n, x in enumerate(every):
        own = jnp.where(lane[0:1] + n * Z < devices, x[6:7], 1.0)
        h = step / own
        parts.append(x[0:1] + h * (x[2:3] + h * (x[3:4] + h * (x[4:5] + h * x[5:6]))))
    ttot = over_all(parts)
    for t in range(2 * SUBSTEPS):
        for cp in halo_copies(t, (0, 1, 2)):
            cp.wait_send()
    for r in range(2):
        for phase in range(2):
            for cp in red_copies(r, phase):
                cp.wait_send()
    l1 = lax.broadcasted_iota(jnp.int32, (1, Z), 1)
    checks[...] = jnp.where(
        l1 == 0, etot / elements, jnp.where(l1 == 1, stot / entries, ttot / elements)
    )


def solution(mesh):
    sizes = tuple(mesh.shape[a] for a in AXES)

    def on_device(displacement, size_field_modes, velocity):
        modes, X, Y, Z = size_field_modes.shape
        assert Y == 2 and displacement.shape == (3, 3 * X, 3 * Y, 3 * Z)
        R, NX, NY = 4 * Y, 3 * X, 3 * Y
        tab = jnp.asarray(row_tables(Y, Z))
        peers = sizes[0] - 1 + sizes[1] * sizes[2] - 1
        groups = -(-sizes[0] * sizes[1] * sizes[2] // Z)
        S = 2 * SUBSTEPS
        vm = lambda *shape: pltpu.VMEM(shape, jnp.float32)
        dma = lambda *shape: pltpu.SemaphoreType.DMA(shape)
        spec = pl.BlockSpec(memory_space=pltpu.VMEM)
        adv, grad, checks = pl.pallas_call(
            functools.partial(kernel, sizes, X, Y, Z),
            out_shape=(
                jax.ShapeDtypeStruct(size_field_modes.shape, jnp.float32),
                jax.ShapeDtypeStruct(displacement.shape, jnp.float32),
                jax.ShapeDtypeStruct((1, Z), jnp.float32),
            ),
            in_specs=[spec] * 4,
            out_specs=(spec,) * 3,
            scratch_shapes=[
                vm(3 * Z, 3 * Z), vm(3 * NX, R, 3 * Z), vm(27, R, Z), vm(27, R, Z), vm(3, R, Z), vm(3, 4, R, Z),
                vm(S, 2, 10, Y, Z), vm(S, 2, 10, Y, Z), vm(S, 2, 10, X, Z), vm(S, 2, 10, X, Z),
                vm(S, 2, R, Z), vm(S, 2, R, Z),
                vm(2, 3, groups, R, Z), vm(2, peers, groups, R, Z),
                vm(3, NX + 1, 4, R, Z), vm(3, NX + 1, 4, R, Z),
                vm(3, 3, NX + 1, 4, R, Z), vm(3, 3, X, 4, 4, R, Z), vm(3, 3, X, 4, 4, R, Z), vm(2, NX + 1, 4, R, Z), vm(X, 4, 4, R, Z), vm(R, Z),
                vm(1, 3, 3, R, Z), vm(1, 3, NX + 1, 3, Z), vm(1, 3, NX + 1, 3, Z), vm(1, R, Z), vm(1, R, Z),
                vm(2, 3, 4, R, Z), vm(2, 3, NX + 1, 4, Z), vm(2, 3, NX + 1, 4, Z), vm(2, R, Z), vm(2, R, Z),
                dma(S, 6), dma(S, 6), dma(2, peers), dma(2, peers), dma(1, 3), dma(1, 3), dma(6), dma(6),
            ],
            compiler_params=pltpu.CompilerParams(collective_id=0, has_side_effects=True),
        )(displacement, size_field_modes, velocity, tab)
        return adv, grad, checks[0, 0:3]

    return jax.shard_map(
        on_device,
        mesh=mesh,
        in_specs=(P(None, "gx", "gy", "gz"),) * 3,
        out_specs=(P(None, "gx", "gy", "gz"), P(None, "gx", "gy", "gz"), P()),
        check_vma=False,
    )
```

profile of v0, /device:TPU:0, one launch (start us, length us, event | category | flops | bytes accessed | tf_op | source)
XLA Modules:
  0.0 64.0 jit_solution(1686484482816151590)
XLA Ops:
  0.6 59.1 %shard_map.67 = (f32[27,2,2,128]{3,2,1,0:T(2,128)}, f32[3,6,6,384]{3,2,1,0:T(8,128)}, f32[1,128]{1,0:T(1,128)}) custom-call(f32[3,6,6,384]{3,2,1,0:T(8,128)} %disp.1, f32[27,2,2,128]{3,2,1,0:T(2,128)} %modes.1, f32[3,2,2,128]{3,2,1,0:T(2,128)} %vel.1, f32[37,8,128]{2,1,0:T(8,128)} %constant.2.clone.tab), custom_call_target="tpu_custom_call" | custom-call | tf_op jit(solution)/shard_map/pallas_call | solution.py:639
  59.8 0.0 copy-start
  59.8 0.7 %copy-done = f32[1,128]{1,0:T(1,128)S(1)} copy-done((f32[1,128]{1,0:T(1,128)S(1)}, f32[1,128]{1,0:T(1,128)}, u32[]{:S(2)}) %copy-start) | copy-done | bytes 536
  60.4 0.5 slice_bitcast_fusion
  60.9 1.4 %copy.9 = f32[27,2,2,128]{3,2,1,0:T(2,128)} copy(f32[27,2,2,128]{3,2,1,0:T(2,128)} %get-tuple-element.12) | data formatting | bytes 110592
  62.4 1.6 %copy.10 = f32[3,6,6,384]{3,2,1,0:T(8,128)} copy(f32[3,6,6,384]{3,2,1,0:T(8,128)} %get-tuple-element.13) | data formatting | bytes 331776
Async XLA Ops:
  59.8 0.7 %copy-start = (f32[1,128]{1,0:T(1,128)S(1)}, f32[1,128]{1,0:T(1,128)}, u32[]{:S(2)}) copy-start(f32[1,128]{1,0:T(1,128)} %get-tuple-element.8) | copy-start | bytes 1540
where the time goes:
time: 64.2 us; the launch traced here: 64 us
  Pallas kernels  59.1 us (92%)
  local copies, waits for them, and re-layouts  4.25 us (7%)
  between operations  0.65 us (1%)
    pallas_call x1, Pallas kernels, on_device(): pl.pallas_call(functools.partial(kernel, sizes, X, Y, Z), out_shape=(jax....  59.1 us
    unnamed x4, local copies, waits for them, and re-layouts  3.74 us

commit v1 on v0

--- a/solution.py
+++ b/solution.py
@@ -73,11 +73,12 @@
     return np.ascontiguousarray(np.broadcast_to(stacked[:, :, None], stacked.shape + (Z,)))
 
 
-def kernel(sizes, X, Y, Z, disp, modes, vel, tab, adv, grad, checks,
-           perm, slab, U, W, VEL, FS, SX, RX, SY, RY, SZ, RZ,
+def kernel(sizes, X, Y, Z, disp_in, modes_in, vel_in, tab, adv, grad, checks,
+           disp, GU, ZP, ZR, ZA, UM, WM, VM, CM, FM, US, WS, VS, CS, FT,
+           perm, slab, U,
            RED, REDR, N, GN, A, G, J, B, SIZ, DT,
            NXR, NYS, NYR, NZS, NZR, FXR, FYS, FYR, FZS, FZR,
-           hs, hr, rs, rr, ns, nr, fs, fr):
+           ls, g1s, g1r, g2s, g2r, zs, zr, y2s, y2r, rs, rr, ns, nr, fs, fr):
     value, slope, legendre, weights = tables_1d()
     NX, NY = 3 * X, 3 * Y
     ROWS = 4 * Y
@@ -92,17 +93,27 @@
         n = sizes[axis]
         return {AXES[axis]: lax.rem(index[axis] + (by + n), n)}
 
+    loads = [
+        pltpu.make_async_copy(modes_in, GU.at[0, 0, 0:27], ls.at[0]),
+        pltpu.make_async_copy(vel_in, GU.at[0, 0, 27:30], ls.at[1]),
+        pltpu.make_async_copy(disp_in, disp, ls.at[2]),
+    ]
+    for cp in loads:
+        cp.start()
     barrier = pltpu.get_barrier_semaphore()
     total = 0
-    moves = [(by, 0, 0) for by in range(1, sizes[0])]
-    moves += [(0, b, c) for b in range(sizes[1]) for c in range(sizes[2]) if b or c]
-    for move in moves:
-        target = {}
-        for axis in range(3):
-            if move[axis]:
-                target.update(at(axis, move[axis]))
-        pl.semaphore_signal(barrier, inc=1, device_id=target, device_id_type=MESH)
-        total += 1
+    for a in range(sizes[0]):
+        for b in range(sizes[1]):
+            for c in range(sizes[2]):
+                move = (a, b, c)
+                if not any(move):
+                    continue
+                target = {}
+                for axis in range(3):
+                    if move[axis]:
+                        target.update(at(axis, move[axis]))
+                pl.semaphore_signal(barrier, inc=1, device_id=target, device_id_type=MESH)
+                total += 1
 
     def copy(src, dst, ss, sr, axis, by):
         return pltpu.make_async_remote_copy(
@@ -110,13 +121,71 @@
             device_id=at(axis, by), device_id_type=MESH,
         )
 
-    U[...] = jnp.zeros_like(U)
-    VEL[...] = jnp.zeros_like(VEL)
+    GX, GY = sizes[0], sizes[1]
+    XG, YG, NS, EDGE = GX * X, GY * Y, GX * X // 2, 2 * SUBSTEPS
+    HALF, FIELDS, SLOTS = Z // 2, 30, Z // EDGE
+
+    def moved(move):
+        target = {}
+        for axis in range(3):
+            if move[axis] % sizes[axis]:
+                target.update(at(axis, move[axis] % sizes[axis] ))
+        return target
+
+    def remote(src, dst, ss, sr, move):
+        return pltpu.make_async_remote_copy(
+            src_ref=src, dst_ref=dst, send_sem=ss, recv_sem=sr,
+            device_id=moved(move), device_id_type=MESH,
+        )
+
+    def plane_copy(ry):
+        return remote(GU.at[0, 0], GU.at[0, ry], g1s.at[ry], g1r.at[ry], (0, -ry, 0))
+
+    def core_copies(ry):
+        return [
+            remote(GU.at[0, ry], GU.at[rx, ry], g2s.at[rx, ry], g2r.at[rx, ry], (-rx, 0, 0))
+            for rx in range(1, GX)
+        ]
+
+    def edge_copies():
+        return [
+            remote(ZP.at[side], ZR.at[0, ry, side], zs.at[side, ry], zr.at[side, ry], (0, -ry, 2 * side - 1))
+            for side in range(2) for ry in range(GY)
+        ]
+
+    def edge_core_copies():
+        return [
+            remote(ZR.at[0], ZR.at[rx], y2s.at[rx], y2r.at[rx], (-rx, 0, 0)) for rx in range(1, GX)
+        ]
+
+    slot2 = lax.broadcasted_iota(jnp.int32, (Y, Z), 1) // EDGE
+    packs = -(-FIELDS * X // SLOTS)
+
+    def pack_edges():
+        acc = [[jnp.zeros((Y, Z), f32) for _ in range(packs)] for _ in range(2)]
+        for m in range(FIELDS):
+            for ix in range(X):
+                t = m * X + ix
+                v, p = t // SLOTS, EDGE * (t % SLOTS)
+                x = GU[0, 0, m, ix]
+                low = pltpu.roll(x, p, 1) if p else x
+                high = pltpu.roll(x, (p + EDGE) % Z, 1) if (p + EDGE) % Z else x
+                acc[0][v] = jnp.where(slot2 == t % SLOTS, low, acc[0][v])
+                acc[1][v] = jnp.where(slot2 == t % SLOTS, high, acc[1][v])
+        for side in range(2):
+            for v in range(packs):
+                ZP[side, v] = acc[side][v]
+
+    for cp in loads[:2]:
+        cp.wait()
+    RED[0, 0] = jnp.zeros_like(RED[0, 0])
+    speed = None
     for ix in range(X):
-        U[:, ix * Y : ix * Y + Y, :] = modes[:, ix]
-        VEL[:, ix * Y : ix * Y + Y, :] = vel[:, ix]
-    RED[0, 0] = jnp.zeros_like(RED[0, 0])
-    RED[0, 0, 0] = jnp.abs(VEL[0]) + jnp.abs(VEL[1]) + jnp.abs(VEL[2])
+        here = jnp.abs(GU[0, 0, 27, ix]) + jnp.abs(GU[0, 0, 28, ix]) + jnp.abs(GU[0, 0, 29, ix])
+        speed = here if speed is None else jnp.maximum(speed, here)
+    RED[0, 0, 0, 0:Y] = speed
+    pack_edges()
+
     def unweave():
         a_i = lax.broadcasted_iota(jnp.int32, (3 * Z, 3 * Z), 0)
         b_i = lax.broadcasted_iota(jnp.int32, (3 * Z, 3 * Z), 1)
@@ -134,7 +203,15 @@
             for k in range(3):
                 N[c, 0:NX, k] = spread[c, :, :, k * Z : (k + 1) * Z]
 
+    loads[2].wait()
+    unweave()
     pl.semaphore_wait(barrier, total)
+    for cp in core_copies(0):
+        cp.start()
+    for ry in range(1, GY):
+        plane_copy(ry).start()
+    for cp in edge_copies():
+        cp.start()
 
     def peers_of(phase):
         if phase == 0:
@@ -208,102 +285,174 @@
                 at_ = c * (NX + 1) + i
                 a[c, i, 3] = jnp.where(lane == Z - 1, packed[:, at_ : at_ + 1], pltpu.roll(a[c, i, 0], Z - 1, 1))
 
-    def halo_copies(s, dims):
-        out = []
-        for d, (sb, rb) in ((0, (SX, RX)), (1, (SY, RY)), (2, (SZ, RZ))):
-            if d not in dims:
-                continue
-            for way in range(2):
-                out.append(copy(sb.at[s, way], rb.at[s, way], hs.at[s, 2 * d + way], hr.at[s, 2 * d + way], d, 1 - 2 * way))
-        return out
-
-    def send_part(s, n, d, tp, tm):
-        if d == 0:
-            SX[s, 0, n] = tp[(X - 1) * Y : EL]
-            SX[s, 1, n] = tm[0:Y]
-        else:
+    scale = [plus_values[m // 9] * plus_values[m // 3 % 3] * plus_values[m % 3] for m in range(27)]
+
+    def assemble():
+        def plane(x, carry):
+            rx, ix = x // X, x % X
+            for ry in range(GY):
+                for m in range(FIELDS):
+                    v = GU[rx, ry, m, ix]
+                    if m < 27:
+                        UM[m, x, ry * Y : ry * Y + Y, :] = scale[m] * v
+                    else:
+                        VM[m - 27, x, ry * Y : ry * Y + Y, :] = v
+            return carry
+
+        lax.fori_loop(0, XG, plane, 0)
+
+    lanes = lax.broadcasted_iota(jnp.int32, (YG, Z), 1)
+    W2, W3 = 2 * EDGE, 3 * EDGE
+
+    def within(lo, hi):
+        return (lanes >= lo) & (lanes < hi)
+
+    def strip_own():
+        def one(q, carry):
+            for m in range(FIELDS):
+                out = jnp.zeros((YG, Z), f32)
+                for h in range(2):
+                    t = UM[m, q + h * NS] if m < 27 else VM[m - 27, q + h * NS]
+                    o = h * HALF
+                    out = jnp.where(within(o, o + W2), pltpu.roll(t, o + W2, 1), out)
+                    out = jnp.where(within(o + 2 * W2, o + 3 * W2), pltpu.roll(t, o + 2 * W2, 1), out)
+                if m < 27:
+                    US[m, q] = out
+                else:
+                    VS[m - 27, q] = out
+            return carry
+
+        lax.fori_loop(0, NS, one, 0)
+
+    def strip_halo():
+        for rx in range(GX):
+            for ry in range(GY):
+                ZA[rx, :, :, ry * Y : ry * Y + Y, :] = ZR[rx, ry]
+        for q in range(NS):
+            for m in range(FIELDS):
+                out = US[m, q] if m < 27 else VS[m - 27, q]
+                for h in range(2):
+                    x = q + h * NS
+                    rx, ix = x // X, x % X
+                    t = m * X + ix
+                    v, p = t // SLOTS, EDGE * (t % SLOTS)
+                    for side in range(2):
+                        o = h * HALF + W2 + side * EDGE
+                        piece = ZA[rx, side, v]
+                        by = (o - p) % Z
+                        piece = pltpu.roll(piece, by, 1) if by else piece
+                        if m < 27:
+                            piece = scale[m] * piece
+                        out = jnp.where(within(o, o + EDGE), piece, out)
+                if m < 27:
+                    US[m, q] = out
+                else:
+                    VS[m - 27, q] = out
+
+    def ynext(t):
+        return pltpu.roll(t, YG - 1, 0)
+
+    def yprev(t):
+        return pltpu.roll(t, 1, 0)
+
+    def znext(t):
+        return pltpu.roll(t, Z - 1, 1)
+
+    def zprev(t):
+        return pltpu.roll(t, 1, 1)
+
+    def coefficients(V, C, nx, wrap):
+        dt = DT[...]
+        for q in range(nx):
+            nxt = V[0, q + 1] if q < nx - 1 else wrap(V[0, 0])
+            for d in range(3):
+                v = V[d, q]
+                ahead = nxt if d == 0 else ynext(v) if d == 1 else znext(v)
+                face = (0.5 * dt) * (v + ahead)
+                C[q, 3 * d] = jnp.maximum(face, 0.0)
+                C[q, 3 * d + 1] = jnp.minimum(face, 0.0)
+                C[q, 3 * d + 2] = (2.0 * dt) * v
+
+    def line(u, hp, hm, v2, ahead, behind):
+        e = u[0] + u[2]
+        up = hp * (e + u[1]) + hm * ahead(e - u[1])
+        low = behind(up)
+        diff = low - up
+        return diff, 3.0 * (v2 * u[0] - (low + up)), 5.0 * (v2 * u[1] + diff)
+
+    def rate(src, C, F, nx, wrap, write):
+        for n in range(9):
+            tp, tm = [], []
+            for q in range(nx):
+                u0, u1, u2 = src[n, q], src[9 + n, q], src[18 + n, q]
+                e = u0 + u2
+                tp.append(e + u1)
+                tm.append(e - u1)
+            for q in range(nx):
+                nxt = tm[q + 1] if q < nx - 1 else wrap(tm[0])
+                f = C[q, 0] * tp[q] + C[q, 1] * nxt
+                F[q + 1, n] = f
+                if q == nx - 1:
+                    F[0, n] = wrap(f)
+
+        def block(q, carry):
+            vx = C[q, 2]
+            for a in range(3):
+                u = [src[9 * a + n, q] for n in range(9)]
+                acc = []
+                for n in range(9):
+                    up, low = F[q + 1, n], F[q, n]
+                    if a == 0:
+                        acc.append(low - up)
+                    elif a == 1:
+                        acc.append(3.0 * (vx * src[n, q] - (low + up)))
+                    else:
+                        acc.append(5.0 * (vx * src[9 + n, q] + (low - up)))
+                for d, st, ot, ahead, behind in ((1, 3, 1, ynext, yprev), (2, 1, 3, znext, zprev)):
+                    hp, hm, v2 = C[q, 3 * d], C[q, 3 * d + 1], C[q, 3 * d + 2]
+                    for o in range(3):
+                        at_ = [ot * o + st * t for t in range(3)]
+                        out = line([u[t] for t in at_], hp, hm, v2, ahead, behind)
+                        for t in range(3):
+                            acc[at_[t]] = acc[at_[t]] + out[t]
+                for n in range(9):
+                    write(9 * a + n, q, acc[n])
+            return carry
+
+        lax.fori_loop(0, nx, block, 0)
+
+    def advance(Ur, Wr, C, F, nx, wrap):
+        def put(m, q, value):
+            Wr[m, q] = value
+
+        def step(m, q, value):
+            Ur[m, q] = (Ur[m, q] + Wr[m, q]) + 0.5 * value
+
+        def substep(t, carry):
+            rate(Ur, C, F, nx, wrap, put)
+            rate(Wr, C, F, nx, wrap, step)
+            return carry
+
+        lax.fori_loop(0, SUBSTEPS, substep, 0)
+
+    def same(t):
+        return t
+
+    def half_turn(t):
+        return pltpu.roll(t, HALF, 1)
+
+    def finish_field():
+        U[...] = jnp.zeros_like(U)
+        for m in range(27):
             for ix in range(X):
-                SY[s, 0, n, ix : ix + 1] = tp[ix * Y + Y - 1 : ix * Y + Y]
-                SY[s, 1, n, ix : ix + 1] = tm[ix * Y : ix * Y + 1]
-
-    def prev_of(d, t, s, n):
-        if d == 0:
-            return jnp.concatenate([RX[s, 0, n], t[: ROWS - Y]], axis=0)
-        if d == 1:
-            parts = []
-            for ix in range(X):
-                parts += [RY[s, 0, n, ix : ix + 1], t[ix * Y : ix * Y + Y - 1]]
-            return jnp.concatenate(parts + [t[EL:]], axis=0)
-        return jnp.where(lane == 0, RZ[s, 0][:, n : n + 1], pltpu.roll(t, 1, 1))
-
-    def next_of(d, t, s, n):
-        if d == 0:
-            return jnp.concatenate([t[Y:EL], RX[s, 1, n], t[EL:]], axis=0)
-        if d == 1:
-            parts = []
-            for ix in range(X):
-                parts += [t[ix * Y + 1 : ix * Y + Y], RY[s, 1, n, ix : ix + 1]]
-            return jnp.concatenate(parts + [t[EL:]], axis=0)
-        return jnp.where(lane == Z - 1, RZ[s, 1][:, n : n + 1], pltpu.roll(t, Z - 1, 1))
-
-    strides = (9, 3, 1)
-    others = [[m for m in range(27) if (m // strides[d]) % 3 == 0] for d in range(3)]
-
-    def rate(src, s, first, between):
-        u = [src[m] for m in range(27)]
-        v = [VEL[d] for d in range(3)]
-        tp, tm = [[], [], []], [[], [], []]
-        for d in (2, 1, 0):
-            for m in others[d]:
-                even = plus_values[0] * u[m] + plus_values[2] * u[m + 2 * strides[d]]
-                odd = plus_values[1] * u[m + strides[d]]
-                tp[d].append(even + odd)
-                tm[d].append(even - odd)
-            ups = tp[d] + [v[d]]
-            lows = tm[d] + [v[d]]
-            if d == 2:
-                up, low = jnp.zeros((ROWS, Z), f32), jnp.zeros((ROWS, Z), f32)
-                for n in range(10 if first else 9):
-                    up = jnp.where(lane == n, ups[n][:, Z - 1 : Z], up)
-                    low = jnp.where(lane == n, lows[n][:, 0:1], low)
-                SZ[s, 0] = up
-                SZ[s, 1] = low
-            else:
-                for n in range(10):
-                    send_part(s, n, d, ups[n], lows[n])
-            for cp in halo_copies(s, (d,)):
-                cp.start()
-        acc = [None] * 27
-        for d in range(3):
-            st = strides[d]
-            va, vb = (2.0 * g10) * v[d], (2.0 * g21) * v[d]
-            for m in others[d]:
-                for mm, term in ((m + st, va * u[m]), (m + 2 * st, vb * u[m + st])):
-                    acc[mm] = term if acc[mm] is None else acc[mm] + term
-        between()
-        for d in range(3):
-            for cp in halo_copies(s, (d,)):
-                cp.wait_recv()
-            if first:
-                high = v[d] + next_of(d, v[d], s, 9)
-                lowf = prev_of(d, v[d], s, 9) + v[d]
-                FS[d, 0] = jnp.maximum(high, 0.0)
-                FS[d, 1] = jnp.minimum(high, 0.0)
-                FS[d, 2] = jnp.maximum(lowf, 0.0)
-                FS[d, 3] = jnp.minimum(lowf, 0.0)
-            st = strides[d]
-            hp, hm, lp, lm = [FS[d, t] for t in range(4)]
-            for n, m in enumerate(others[d]):
-                hi = hp * tp[d][n] + hm * next_of(d, tm[d][n], s, n)
-                lo = lp * prev_of(d, tp[d][n], s, n) + lm * tm[d][n]
-                diff, both = lo - hi, lo + hi
-                for mm, term in (
-                    (m, plus_values[0] * diff),
-                    (m + st, (-plus_values[1]) * both),
-                    (m + 2 * st, plus_values[2] * diff),
-                ):
-                    acc[mm] = term if acc[mm] is None else acc[mm] + term
-        return acc
+                t = UM[m, ix]
+                h, q = ix // NS, ix % NS
+                s = US[m, q]
+                o = h * HALF
+                left = pltpu.roll(s, (Z - o - 2 * W2) % Z, 1)
+                right = pltpu.roll(s, (Z - W2 - o) % Z, 1)
+                t = jnp.where(lanes < EDGE, left, jnp.where(lanes >= Z - EDGE, right, t))
+                U[m, ix * Y : ix * Y + Y, :] = (1.0 / scale[m]) * t[0:Y]
 
     def yz_of(src):
         def yz(i, carry):
@@ -339,60 +488,50 @@
                     J[d, c, ix, p, r] = jac + 1.0 if c == d else jac
 
     red_start(0, 0)
-
-    def between_0():
-        red_finish(0, 0, jnp.maximum)
-        red_start(0, 1)
-        unweave()
-        rim_x(N, 0).start()
-
-    def between_1():
-        rim_x(N, 0).wait()
-        rim_y_pack(N, 0)
-        rim_y(0).start()
-        red_finish(0, 1, jnp.maximum)
-
-    def between_2():
-        rim_y(0).wait()
-        rim_y_unpack(N, 0)
-        rim_z_pack(N, 0)
-        rim_z(0).start()
-
-    def between_3():
-        rim_z(0).wait()
-        rim_z_unpack(N, 0)
-        yz_of(N)
-
-    def two_stages(s, first, between_a, between_b, dt_of):
-        w = rate(U, s, first, between_a)
-        for m in range(27):
-            W[m] = w[m]
-        w = rate(W, s + 1, False, between_b)
-        dt = dt_of()
-        half = 0.5 * dt * dt
-        for m in range(27):
-            U[m] = U[m] + dt * W[m] + half * w[m]
-
-    def time_step():
-        fastest = jnp.max(RED[0, 2, 0], axis=(0, 1), keepdims=True)
-        DT[...] = jnp.broadcast_to(courant / jnp.maximum(fastest, 0.25), (ROWS, Z))
-        return DT[...]
-
-    two_stages(0, True, between_0, between_1, time_step)
-    two_stages(2, False, between_2, between_3, lambda: DT[...])
-    units = (4 * X) // (2 * SUBSTEPS - 4)
-
-    def substep(t, carry):
-        def some(s):
-            def run():
-                for n in range(units):
-                    jacobians((s - 4) * units + n)
-            return run
-
-        two_stages(2 * t, False, some(2 * t), some(2 * t + 1), lambda: DT[...])
+    rim_x(N, 0).start()
+    rim_x(N, 0).wait()
+    rim_y_pack(N, 0)
+    rim_y(0).start()
+    red_finish(0, 0, jnp.maximum)
+    red_start(0, 1)
+    for ry in range(1, GY):
+        plane_copy(ry).wait_recv()
+        for cp in core_copies(ry):
+            cp.start()
+    rim_y(0).wait()
+    rim_y_unpack(N, 0)
+    rim_z_pack(N, 0)
+    rim_z(0).start()
+    for cp in edge_copies():
+        cp.wait_recv()
+    for cp in edge_core_copies():
+        cp.start()
+    red_finish(0, 1, jnp.maximum)
+    fastest = jnp.max(RED[0, 2, 0], axis=(0, 1), keepdims=True)
+    DT[...] = jnp.broadcast_to(courant / jnp.maximum(fastest, 0.25), (YG, Z))
+    for ry in range(GY):
+        for cp in core_copies(ry):
+            cp.wait_recv()
+    assemble()
+    strip_own()
+    coefficients(VM, CM, XG, same)
+    advance(UM, WM, CM, FM, XG, same)
+    for cp in edge_core_copies():
+        cp.wait_recv()
+    strip_halo()
+    coefficients(VS, CS, NS, half_turn)
+    advance(US, WS, CS, FT, NS, half_turn)
+    finish_field()
+    rim_z(0).wait()
+    rim_z_unpack(N, 0)
+    yz_of(N)
+
+    def all_jacobians(t, carry):
+        jacobians(t)
         return carry
 
-    lax.fori_loop(2, SUBSTEPS, substep, 0)
+    lax.fori_loop(0, 4 * X, all_jacobians, 0)
+
     def size_of(ix, carry):
         mid = {}
         for a in range(3):
@@ -609,9 +748,13 @@
         h = step / own
         parts.append(x[0:1] + h * (x[2:3] + h * (x[3:4] + h * (x[4:5] + h * x[5:6]))))
     ttot = over_all(parts)
-    for t in range(2 * SUBSTEPS):
-        for cp in halo_copies(t, (0, 1, 2)):
+    for ry in range(GY):
+        if ry:
+            plane_copy(ry).wait_send()
+        for cp in core_copies(ry):
             cp.wait_send()
+    for cp in edge_copies() + edge_core_copies():
+        cp.wait_send()
     for r in range(2):
         for phase in range(2):
             for cp in red_copies(r, phase):
@@ -632,7 +775,10 @@
         tab = jnp.asarray(row_tables(Y, Z))
         peers = sizes[0] - 1 + sizes[1] * sizes[2] - 1
         groups = -(-sizes[0] * sizes[1] * sizes[2] // Z)
-        S = 2 * SUBSTEPS
+        GX, GY = sizes[0], sizes[1]
+        XG, YG, NS = GX * X, GY * Y, GX * X // 2
+        packs = -(-30 * X // (Z // (2 * SUBSTEPS)))
+        assert YG == 8 and XG % 2 == 0 and min(sizes) > 1
         vm = lambda *shape: pltpu.VMEM(shape, jnp.float32)
         dma = lambda *shape: pltpu.SemaphoreType.DMA(shape)
         spec = pl.BlockSpec(memory_space=pltpu.VMEM)
@@ -643,18 +789,19 @@
                 jax.ShapeDtypeStruct(displacement.shape, jnp.float32),
                 jax.ShapeDtypeStruct((1, Z), jnp.float32),
             ),
-            in_specs=[spec] * 4,
+            in_specs=[pl.BlockSpec(memory_space=pl.ANY)] * 3 + [spec],
             out_specs=(spec,) * 3,
             scratch_shapes=[
-                vm(3 * Z, 3 * Z), vm(3 * NX, R, 3 * Z), vm(27, R, Z), vm(27, R, Z), vm(3, R, Z), vm(3, 4, R, Z),
-                vm(S, 2, 10, Y, Z), vm(S, 2, 10, Y, Z), vm(S, 2, 10, X, Z), vm(S, 2, 10, X, Z),
-                vm(S, 2, R, Z), vm(S, 2, R, Z),
+                vm(3, NX, NY, 3 * Z), vm(GX, GY, 30, X, Y, Z), vm(2, packs, Y, Z), vm(GX, GY, 2, packs, Y, Z), vm(GX, 2, packs, YG, Z),
+                vm(27, XG, YG, Z), vm(27, XG, YG, Z), vm(3, XG, YG, Z), vm(XG, 9, YG, Z), vm(XG + 1, 9, YG, Z),
+                vm(27, NS, YG, Z), vm(27, NS, YG, Z), vm(3, NS, YG, Z), vm(NS, 9, YG, Z), vm(NS + 1, 9, YG, Z),
+                vm(3 * Z, 3 * Z), vm(3 * NX, R, 3 * Z), vm(27, R, Z),
                 vm(2, 3, groups, R, Z), vm(2, peers, groups, R, Z),
                 vm(3, NX + 1, 4, R, Z), vm(3, NX + 1, 4, R, Z),
                 vm(3, 3, NX + 1, 4, R, Z), vm(3, 3, X, 4, 4, R, Z), vm(3, 3, X, 4, 4, R, Z), vm(2, NX + 1, 4, R, Z), vm(X, 4, 4, R, Z), vm(R, Z),
                 vm(1, 3, 3, R, Z), vm(1, 3, NX + 1, 3, Z), vm(1, 3, NX + 1, 3, Z), vm(1, R, Z), vm(1, R, Z),
                 vm(2, 3, 4, R, Z), vm(2, 3, NX + 1, 4, Z), vm(2, 3, NX + 1, 4, Z), vm(2, R, Z), vm(2, R, Z),
-                dma(S, 6), dma(S, 6), dma(2, peers), dma(2, peers), dma(1, 3), dma(1, 3), dma(6), dma(6),
+                dma(3), dma(GY), dma(GY), dma(GX, GY), dma(GX, GY), dma(2, GY), dma(2, GY), dma(GX), dma(GX), dma(2, peers), dma(2, peers), dma(1, 3), dma(1, 3), dma(6), dma(6),
             ],
             compiler_params=pltpu.CompilerParams(collective_id=0, has_side_effects=True),
         )(displacement, size_field_modes, velocity, tab)

time: 64.2 us -> 52 us (0.81)
  Pallas kernels: 59.1 us -> 46.9 us
    pallas_call x1, Pallas kernels: 59.1 us -> 46.9 us  [on_device(): pl.pallas_call(functools.partial(kernel, sizes, X, Y, Z), out_shape=(jax....]
where the time goes in v1:
time: 52 us; the launch traced here: 51.8 us
  Pallas kernels  46.9 us (90%)
  local copies, waits for them, and re-layouts  4.25 us (8%)
  between operations  0.65 us (1%)
    pallas_call x1, Pallas kernels, on_device(): pl.pallas_call(functools.partial(kernel, sizes, X, Y, Z), out_shape=(jax....  46.9 us
    unnamed x4, local copies, waits for them, and re-layouts  3.74 us

profile of v1, /device:TPU:0, one launch (start us, length us, event | category | flops | bytes accessed | tf_op | source)
XLA Modules:
  0.0 51.8 jit_solution(2608345396690114563)
XLA Ops:
  0.6 46.9 %shard_map.67 = (f32[27,2,2,128]{3,2,1,0:T(2,128)}, f32[3,6,6,384]{3,2,1,0:T(8,128)}, f32[1,128]{1,0:T(1,128)}) custom-call(f32[3,6,6,384]{3,2,1,0:T(8,128)} %disp_in.1, f32[27,2,2,128]{3,2,1,0:T(2,128)} %modes_in.1, f32[3,2,2,128]{3,2,1,0:T(2,128)} %vel_in.1, f32[37,8,128]{2,1,0:T(8,128)} %constant.2.clone.tab), custom_call_target="tpu_custom_call" | custom-call | tf_op jit(solution)/shard_map/pallas_call | solution.py:785
  47.5 0.0 copy-start
  47.6 0.7 %copy-done = f32[1,128]{1,0:T(1,128)S(1)} copy-done((f32[1,128]{1,0:T(1,128)S(1)}, f32[1,128]{1,0:T(1,128)}, u32[]{:S(2)}) %copy-start) | copy-done | bytes 536
  48.2 0.5 slice_bitcast_fusion
  48.7 1.4 %copy.9 = f32[27,2,2,128]{3,2,1,0:T(2,128)} copy(f32[27,2,2,128]{3,2,1,0:T(2,128)} %get-tuple-element.12) | data formatting | bytes 110592
  50.2 1.6 %copy.10 = f32[3,6,6,384]{3,2,1,0:T(8,128)} copy(f32[3,6,6,384]{3,2,1,0:T(8,128)} %get-tuple-element.13) | data formatting | bytes 331776
Async XLA Ops:
  47.5 0.7 %copy-start = (f32[1,128]{1,0:T(1,128)S(1)}, f32[1,128]{1,0:T(1,128)}, u32[]{:S(2)}) copy-start(f32[1,128]{1,0:T(1,128)} %get-tuple-element.8) | copy-start | bytes 1540

commit v2 on v1

--- a/solution.py
+++ b/solution.py
@@ -75,19 +75,18 @@
 
 def kernel(sizes, X, Y, Z, disp_in, modes_in, vel_in, tab, adv, grad, checks,
            disp, GU, ZP, ZR, ZA, UM, WM, VM, CM, FM, US, WS, VS, CS, FT,
-           perm, slab, U,
-           RED, REDR, N, GN, A, G, J, B, SIZ, DT,
-           NXR, NYS, NYR, NZS, NZR, FXR, FYS, FYR, FZS, FZR,
+           perm, slab, U, ROWS, N, GN, A, G, J, B, SIZ, DT,
+           NXR, NYS, NYR, NXYR, NZS, NZR, FXR, FYS, FYR, FXYR, FZS, FZR, FES, FER,
            ls, g1s, g1r, g2s, g2r, zs, zr, y2s, y2r, rs, rr, ns, nr, fs, fr):
     value, slope, legendre, weights = tables_1d()
     NX, NY = 3 * X, 3 * Y
-    ROWS = 4 * Y
+    ROWS_Y = 4 * Y
     EL = X * Y
     f32 = jnp.float32
     index = [lax.axis_index(a) for a in AXES]
-    lane = lax.broadcasted_iota(jnp.int32, (ROWS, Z), 1)
-    row = lax.broadcasted_iota(jnp.int32, (ROWS, Z), 0)
-    oTV, oTD, oGV, oGD, oL, oW = 0, NY + 1, 2 * NY + 2, 2 * NY + 2 + ROWS, 2 * NY + 2 + 2 * ROWS, 2 * NY + 2 + 2 * ROWS + 3 * Y
+    lane = lax.broadcasted_iota(jnp.int32, (ROWS_Y, Z), 1)
+    row = lax.broadcasted_iota(jnp.int32, (ROWS_Y, Z), 0)
+    oTV, oTD, oGV, oGD, oL, oW = 0, NY + 1, 2 * NY + 2, 2 * NY + 2 + ROWS_Y, 2 * NY + 2 + 2 * ROWS_Y, 2 * NY + 2 + 2 * ROWS_Y + 3 * Y
 
     def at(axis, by):
         n = sizes[axis]
@@ -178,12 +177,11 @@
 
     for cp in loads[:2]:
         cp.wait()
-    RED[0, 0] = jnp.zeros_like(RED[0, 0])
     speed = None
     for ix in range(X):
         here = jnp.abs(GU[0, 0, 27, ix]) + jnp.abs(GU[0, 0, 28, ix]) + jnp.abs(GU[0, 0, 29, ix])
         speed = here if speed is None else jnp.maximum(speed, here)
-    RED[0, 0, 0, 0:Y] = speed
+    ROWS[0, 0] = jnp.broadcast_to(jnp.max(speed, axis=0, keepdims=True), (2, Z))
     pack_edges()
 
     def unweave():
@@ -196,9 +194,9 @@
             for i in range(NX):
                 slab[c * NX + i, 0:NY, :] = disp[c, i]
         spread = jnp.dot(
-            slab[...].reshape(3 * NX * ROWS, 3 * Z), perm[...],
+            slab[...].reshape(3 * NX * ROWS_Y, 3 * Z), perm[...],
             precision=lax.Precision.HIGHEST, preferred_element_type=f32,
-        ).reshape(3, NX, ROWS, 3 * Z)
+        ).reshape(3, NX, ROWS_Y, 3 * Z)
         for c in range(3):
             for k in range(3):
                 N[c, 0:NX, k] = spread[c, :, :, k * Z : (k + 1) * Z]
@@ -213,77 +211,75 @@
     for cp in edge_copies():
         cp.start()
 
-    def peers_of(phase):
-        if phase == 0:
-            return [(by, 0, 0) for by in range(1, sizes[0])]
-        return [(0, b, c) for b in range(sizes[1]) for c in range(sizes[2]) if b or c]
-
-    def red_copies(r, phase):
-        off = 0 if phase == 0 else sizes[0] - 1
-        out = []
-        for n, move in enumerate(peers_of(phase)):
-            target = {}
-            for axis in range(3):
-                if move[axis]:
-                    target.update(at(axis, move[axis]))
-            out.append(pltpu.make_async_remote_copy(
-                src_ref=RED.at[r, phase], dst_ref=REDR.at[r, off + n],
-                send_sem=rs.at[r, off + n], recv_sem=rr.at[r, off + n],
-                device_id=target, device_id_type=MESH,
-            ))
+    devices = sizes[0] * sizes[1] * sizes[2]
+    stages = [(0, 1, 2)] if devices <= 64 else [(0,), (1, 2)]
+
+    def row_stage(r, stage):
+        block = 1
+        for axes in stages[:stage]:
+            for axis in axes:
+                block *= sizes[axis]
+        moves = [()]
+        for axis in range(3):
+            moves = [m + (b,) for m in moves for b in range(sizes[axis] if axis in stages[stage] else 1)]
+        src = ROWS.at[r, 0:block]
+        copies = [
+            remote(src, ROWS.at[r, n * block : (n + 1) * block], rs.at[r, stage], rr.at[r, stage], m)
+            for n, m in enumerate(moves) if n
+        ]
+        rest = ROWS.at[r, block : len(moves) * block]
+        return copies, remote(rest, rest, rs.at[r, stage], rr.at[r, stage], moves[1])
+
+    def rows_start(r, stage):
+        for cp in row_stage(r, stage)[0]:
+            cp.start()
+
+    def rows_finish(r):
+        for stage in range(len(stages)):
+            row_stage(r, stage)[1].wait_recv()
+            if stage + 1 < len(stages):
+                rows_start(r, stage + 1)
+
+    def rows_sent(r):
+        for stage in range(len(stages)):
+            row_stage(r, stage)[1].wait_send()
+
+    in_lane = lambda n: functools.reduce(jnp.logical_or, [lane == c * (NX + 1) + n for c in range(3)])
+
+    def rim_copies():
+        out = [
+            remote(N.at[:, 0, 0:3], NXR, ns.at[0], nr.at[0], (-1, 0, 0)),
+            remote(NYS, NYR, ns.at[1], nr.at[1], (0, -1, 0)),
+            remote(NYS.at[:, 0], NXYR, ns.at[2], nr.at[2], (-1, -1, 0)),
+        ]
+        for n, move in enumerate(((0, 0, -1), (-1, 0, -1), (0, -1, -1), (-1, -1, -1))):
+            out.append(remote(NZS, NZR.at[n], ns.at[3 + n], nr.at[3 + n], move))
         return out
 
-    def red_start(r, phase):
-        for cp in red_copies(r, phase):
-            cp.start()
-
-    def red_finish(r, phase, op):
-        off = 0 if phase == 0 else sizes[0] - 1
-        copies = red_copies(r, phase)
-        for cp in copies:
-            cp.wait_recv()
-        total = RED[r, phase]
-        for n in range(len(copies)):
-            total = op(total, REDR[r, off + n])
-        RED[r, phase + 1] = total
-
-    def rim_x(a, t):
-        return copy(a.at[:, 0, 0:3], NXR.at[t], ns.at[t, 0], nr.at[t, 0], 0, -1)
-
-    def rim_y(t):
-        return copy(NYS.at[t], NYR.at[t], ns.at[t, 1], nr.at[t, 1], 1, -1)
-
-    def rim_y_pack(a, t):
+    def rim_pack():
+        packed = jnp.zeros((ROWS_Y, Z), f32)
+        for c in range(3):
+            for i in range(NX):
+                for k in range(3):
+                    NYS[c, i, k : k + 1, :] = N[c, i, k, 0:1, :]
+                packed = jnp.where(lane == c * (NX + 1) + i, N[c, i, 0][:, 0:1], packed)
+        NZS[...] = packed
+
+    def rim_unpack():
         for c in range(3):
             for k in range(3):
-                a[c, NX, k] = NXR[t, c, k]
-        for c in range(3):
-            for i in range(NX + 1):
-                for k in range(3):
-                    NYS[t, c, i, k : k + 1, :] = a[c, i, k, 0:1, :]
-
-    def rim_y_unpack(a, t):
-        for c in range(3):
-            for i in range(NX + 1):
-                for k in range(3):
-                    a[c, i, k, NY : NY + 1, :] = NYR[t, c, i, k : k + 1, :]
-
-    def rim_z(t):
-        return copy(NZS.at[t], NZR.at[t], ns.at[t, 2], nr.at[t, 2], 2, -1)
-
-    def rim_z_pack(a, t):
-        packed = jnp.zeros((ROWS, Z), f32)
-        for c in range(3):
-            for i in range(NX + 1):
-                packed = jnp.where(lane == c * (NX + 1) + i, a[c, i, 0][:, 0:1], packed)
-        NZS[t] = packed
-
-    def rim_z_unpack(a, t):
-        packed = NZR[t]
+                N[c, NX, k] = NXR[c, k]
+                N[c, NX, k, NY : NY + 1, :] = NXYR[c, k : k + 1, :]
+                for i in range(NX):
+                    N[c, i, k, NY : NY + 1, :] = NYR[c, i, k : k + 1, :]
+        last = in_lane(NX)
+        packed = jnp.where(last, pltpu.roll(NZR[1], NX, 1), NZR[0])
+        below = jnp.where(last[0:1], pltpu.roll(NZR[3], NX, 1)[0:1], NZR[2][0:1])
+        packed = jnp.where(row == NY, jnp.broadcast_to(below, (ROWS_Y, Z)), packed)
         for c in range(3):
             for i in range(NX + 1):
                 at_ = c * (NX + 1) + i
-                a[c, i, 3] = jnp.where(lane == Z - 1, packed[:, at_ : at_ + 1], pltpu.roll(a[c, i, 0], Z - 1, 1))
+                N[c, i, 3] = jnp.where(lane == Z - 1, packed[:, at_ : at_ + 1], pltpu.roll(N[c, i, 0], Z - 1, 1))
 
     scale = [plus_values[m // 9] * plus_values[m // 3 % 3] * plus_values[m % 3] for m in range(27)]
 
@@ -419,7 +415,11 @@
                     write(9 * a + n, q, acc[n])
             return carry
 
-        lax.fori_loop(0, nx, block, 0)
+        if nx <= 4:
+            for q in range(nx):
+                block(q, 0)
+        else:
+            lax.fori_loop(0, nx, block, 0)
 
     def advance(Ur, Wr, C, F, nx, wrap):
         def put(m, q, value):
@@ -487,27 +487,31 @@
                     jac = slope_at(ix, p, r, c, d)
                     J[d, c, ix, p, r] = jac + 1.0 if c == d else jac
 
-    red_start(0, 0)
-    rim_x(N, 0).start()
-    rim_x(N, 0).wait()
-    rim_y_pack(N, 0)
-    rim_y(0).start()
-    red_finish(0, 0, jnp.maximum)
-    red_start(0, 1)
+    rows_start(0, 0)
+    rim_pack()
+    for cp in rim_copies():
+        cp.start()
     for ry in range(1, GY):
         plane_copy(ry).wait_recv()
         for cp in core_copies(ry):
             cp.start()
-    rim_y(0).wait()
-    rim_y_unpack(N, 0)
-    rim_z_pack(N, 0)
-    rim_z(0).start()
     for cp in edge_copies():
         cp.wait_recv()
     for cp in edge_core_copies():
         cp.start()
-    red_finish(0, 1, jnp.maximum)
-    fastest = jnp.max(RED[0, 2, 0], axis=(0, 1), keepdims=True)
+    for cp in rim_copies():
+        cp.wait()
+    rim_unpack()
+    yz_of(N)
+
+    def all_jacobians(t, carry):
+        jacobians(t)
+        return carry
+
+    lax.fori_loop(0, 4 * X, all_jacobians, 0)
+    rows_finish(0)
+    fastest = functools.reduce(jnp.maximum, [ROWS[0, n] for n in range(devices)])
+    fastest = jnp.max(fastest, axis=(0, 1), keepdims=True)
     DT[...] = jnp.broadcast_to(courant / jnp.maximum(fastest, 0.25), (YG, Z))
     for ry in range(GY):
         for cp in core_copies(ry):
@@ -522,16 +526,6 @@
     coefficients(VS, CS, NS, half_turn)
     advance(US, WS, CS, FT, NS, half_turn)
     finish_field()
-    rim_z(0).wait()
-    rim_z_unpack(N, 0)
-    yz_of(N)
-
-    def all_jacobians(t, carry):
-        jacobians(t)
-        return carry
-
-    lax.fori_loop(0, 4 * X, all_jacobians, 0)
-
     def size_of(ix, carry):
         mid = {}
         for a in range(3):
@@ -588,7 +582,7 @@
                     G[d, c, ix, p, r] = scale * g
         return esum
 
-    zero = jnp.zeros((ROWS, Z), f32)
+    zero = jnp.zeros((ROWS_Y, Z), f32)
     esum = lax.fori_loop(0, 4 * X, gauss, zero)
 
     def back_c(c, carry):
@@ -618,7 +612,7 @@
         for i in range(NX + 1):
             for k in range(4):
                 acc = None
-                for s in range(ROWS):
+                for s in range(ROWS_Y):
                     term = tab[oGV + s] * B[0, i, k, s : s + 1, :] + tab[oGD + s] * B[1, i, k, s : s + 1, :]
                     acc = term if acc is None else acc + term
                 GN[c, i, k] = acc
@@ -626,49 +620,89 @@
 
     lax.fori_loop(0, 3, back_c, 0)
 
-    def both_ways(src_up, src_down, axis, slot, up, down):
-        copies = [
-            copy(src_up, up, fs.at[slot], fr.at[slot], axis, 1),
-            copy(src_down, down, fs.at[slot + 1], fr.at[slot + 1], axis, -1),
-        ]
-        for cp in copies:
-            cp.start()
-        for cp in copies:
-            cp.wait()
-
-    up, down = zero, zero
+    def row_of(column_of):
+        out = zero
+        for c in range(3):
+            out = jnp.where(lane == c * ROWS_Y + row, column_of(c), out)
+        return jnp.sum(out, axis=0, keepdims=True)
+
+    far, near = zero, zero
     for c in range(3):
         for i in range(NX + 1):
             here = lane == c * (NX + 1) + i
-            up = jnp.where(here, GN[c, i, 3][:, Z - 1 : Z], up)
-            down = jnp.where(here, GN[c, i, 0][:, 0:1], down)
-    FZS[0] = up
-    FZS[1] = down
-    both_ways(FZS.at[0], FZS.at[1], 2, 0, FZR.at[0], FZR.at[1])
-    up, down = FZR[0], FZR[1]
+            far = jnp.where(here, GN[c, i, 3][:, Z - 1 : Z], far)
+            near = jnp.where(here, GN[c, i, 0][:, 0:1], near)
+    FZS[0] = far
+    FZS[1] = near
+    for zs_, (k, at_) in enumerate(((3, Z - 1), (0, 0))):
+        for xs_, i in enumerate((NX, 0)):
+            FES[zs_, xs_] = row_of(lambda c: GN[c, i, k][:, at_ : at_ + 1])
+        for ys_, j in enumerate((NY, 0)):
+            FES[zs_, 2 + ys_] = FZS[zs_][j : j + 1]
     for c in range(3):
         for i in range(NX + 1):
-            n = c * (NX + 1) + i
-            g0, g3 = GN[c, i, 0], GN[c, i, 3]
-            full = g0 + jnp.where(lane == 0, up[:, n : n + 1], pltpu.roll(g3, 1, 1))
-            GN[c, i, 0] = full
-            GN[c, i, 3] = jnp.where(lane == Z - 1, g3 + down[:, n : n + 1], pltpu.roll(full, Z - 1, 1))
-    both_ways(GN.at[:, NX], GN.at[:, 0], 0, 2, FXR.at[0], FXR.at[1])
-    for c in range(3):
-        for k in range(4):
-            GN[c, 0, k] = GN[c, 0, k] + FXR[0, c, k]
-            GN[c, NX, k] = GN[c, NX, k] + FXR[1, c, k]
-    for c in range(3):
-        for i in range(NX + 1):
+            GN[c, i, 0] = GN[c, i, 0] + jnp.where(lane == 0, 0.0, pltpu.roll(GN[c, i, 3], 1, 1))
             for k in range(4):
                 FYS[0, c, i, k : k + 1, :] = GN[c, i, k, NY : NY + 1, :]
                 FYS[1, c, i, k : k + 1, :] = GN[c, i, k, 0:1, :]
-    both_ways(FYS.at[0], FYS.at[1], 1, 4, FYR.at[0], FYR.at[1])
+    ways = (1, -1)
+
+    def fold_copies():
+        out = []
+
+        def add(src, dst, move):
+            n = len(out)
+            out.append(remote(src, dst, fs.at[n], fr.at[n], move))
+
+        for zs_ in range(2):
+            for xs_ in range(2):
+                for ys_ in range(2):
+                    add(FES.at[zs_, xs_], FER.at[zs_, 4 + 2 * xs_ + ys_], (ways[xs_], ways[ys_], ways[zs_]))
+            for ys_ in range(2):
+                add(FES.at[zs_, 2 + ys_], FER.at[zs_, 2 + ys_], (0, ways[ys_], ways[zs_]))
+            for xs_ in range(2):
+                add(FES.at[zs_, xs_], FER.at[zs_, xs_], (ways[xs_], 0, ways[zs_]))
+            add(FZS.at[zs_], FZR.at[zs_], (0, 0, ways[zs_]))
+        for ys_ in range(2):
+            for xs_ in range(2):
+                add(FYS.at[ys_, :, (NX, 0)[xs_]], FXYR.at[xs_, ys_], (ways[xs_], ways[ys_], 0))
+            add(FYS.at[ys_], FYR.at[ys_], (0, ways[ys_], 0))
+        for xs_ in range(2):
+            add(GN.at[:, (NX, 0)[xs_]], FXR.at[xs_], (ways[xs_], 0, 0))
+        return out
+
+    for cp in fold_copies():
+        cp.start()
+    for cp in fold_copies():
+        cp.wait()
+
+    lane1, row_j = lane[0:1], lane[0:1] % ROWS_Y
+    planes = []
+    for zs_ in range(2):
+        p = FZR[zs_]
+        p = p + jnp.where(row == 0, FER[zs_, 2], 0.0) + jnp.where(row == NY, FER[zs_, 3], 0.0)
+        for xs_, i in enumerate((0, NX)):
+            edge = FER[zs_, xs_]
+            edge = edge + jnp.where(row_j == 0, pltpu.roll(FER[zs_, 4 + 2 * xs_], Z - NY, 1), 0.0)
+            edge = edge + jnp.where(row_j == NY, pltpu.roll(FER[zs_, 5 + 2 * xs_], NY, 1), 0.0)
+            for c in range(3):
+                col = jnp.sum(jnp.where(lane == c * ROWS_Y + row, edge, 0.0), axis=1, keepdims=True)
+                p = p + jnp.where(lane == c * (NX + 1) + i, col, 0.0)
+        planes.append(p)
     for c in range(3):
+        for k in range(4):
+            for xs_, i in enumerate((0, NX)):
+                GN[c, i, k] = GN[c, i, k] + FXR[xs_, c, k]
+                for ys_, j in enumerate((0, NY)):
+                    GN[c, i, k, j : j + 1, :] = GN[c, i, k, j : j + 1, :] + FXYR[xs_, ys_, c, k : k + 1, :]
+            for i in range(NX + 1):
+                for ys_, j in enumerate((0, NY)):
+                    GN[c, i, k, j : j + 1, :] = GN[c, i, k, j : j + 1, :] + FYR[ys_, c, i, k : k + 1, :]
         for i in range(NX + 1):
-            for k in range(4):
-                GN[c, i, k, 0:1, :] = GN[c, i, k, 0:1, :] + FYR[0, c, i, k : k + 1, :]
-                GN[c, i, k, NY : NY + 1, :] = GN[c, i, k, NY : NY + 1, :] + FYR[1, c, i, k : k + 1, :]
+            n = c * (NX + 1) + i
+            full = GN[c, i, 0] + jnp.where(lane == 0, planes[0][:, n : n + 1], 0.0)
+            GN[c, i, 0] = full
+            GN[c, i, 3] = jnp.where(lane == Z - 1, GN[c, i, 3] + planes[1][:, n : n + 1], pltpu.roll(full, Z - 1, 1))
     ssum = zero
     for c in range(3):
         for i in range(NX):
@@ -676,17 +710,16 @@
                 g = GN[c, i, k]
                 ssum = ssum + g * g
     ssum = jnp.where(row < NY, ssum, 0.0)
-    devices = sizes[0] * sizes[1] * sizes[2]
     elements = float(EL * Z * devices)
     entries = 81.0 * elements
     mine = jnp.sum(ssum, axis=(0, 1), keepdims=True)
     bound = trial_step / jnp.sqrt(1.0 + mine / entries)
-    bound = jnp.broadcast_to(bound, (ROWS, Z))
+    bound = jnp.broadcast_to(bound, (ROWS_Y, Z))
     yz_of(GN)
 
     def trial(t, sums):
         ix, r = t // 4, t % 4
-        s1, s2, s3, s4 = sums
+        s2, s3, s4 = sums
         for p in range(4):
             size = SIZ[ix, p, r]
             inv = 1.0 / size
@@ -694,7 +727,7 @@
             M = [[J[d, c, ix, p, r] * inv for d in range(3)] for c in range(3)]
             K = [[slope_at(ix, p, r, c, d) * move for d in range(3)] for c in range(3)]
             w = wrow * (gauss_weight(r) * float(weights[p])) * (size * size * size)
-            q = [None] * 4
+            q = [None] * 3
             for d, e in pairs:
                 d0 = dot3(M, M, d, e)
                 d2 = dot3(K, K, d, e)
@@ -703,51 +736,49 @@
                     d1 = 2.0 * dot3(M, K, d, d)
                 else:
                     d1 = dot3(M, K, d, e) + dot3(K, M, d, e)
-                terms = [2.0 * (d0 * d1), d1 * d1 + 2.0 * (d0 * d2), 2.0 * (d1 * d2), d2 * d2]
-                for n in range(4):
+                terms = [d1 * d1 + 2.0 * (d0 * d2), 2.0 * (d1 * d2), d2 * d2]
+                for n in range(3):
                     term = terms[n] if d == e else 2.0 * terms[n]
                     q[n] = term if q[n] is None else q[n] + term
-            s1, s2, s3, s4 = s1 + w * q[0], s2 + w * q[1], s3 + w * q[2], s4 + w * q[3]
-        return s1, s2, s3, s4
-
-    sums = lax.fori_loop(0, 4 * X, trial, (zero,) * 4)
+            s2, s3, s4 = s2 + w * q[0], s3 + w * q[1], s4 + w * q[2]
+        return s2, s3, s4
+
+    sums = lax.fori_loop(0, 4 * X, trial, (zero,) * 3)
     block = zero
     for n, part in enumerate((esum, ssum) + tuple(sums)):
         block = jnp.where(row == n, jnp.sum(part, axis=0, keepdims=True), block)
     column = jnp.sum(block, axis=1, keepdims=True)
-    column = jnp.where(row == 6, bound, jnp.broadcast_to(column, (ROWS, Z)))
-    me = (index[0] * sizes[1] + index[1]) * sizes[2] + index[2]
-    groups = RED.shape[2]
-    for n in range(groups):
-        RED[1, 0, n] = jnp.where(lane + n * Z == me, column, 0.0)
-    red_start(1, 0)
+    ROWS[1, 0, 0:1] = jnp.sum(jnp.where(lane == row, column, 0.0), axis=0, keepdims=True)
+    ROWS[1, 0, 1:2] = 1.0 / bound[0:1]
+    rows_start(1, 0)
     for c in range(3):
         for k in range(3):
             slab[c * NX : (c + 1) * NX, :, k * Z : (k + 1) * Z] = GN[c, 0:NX, k]
-    red_finish(1, 0, jnp.add)
-    red_start(1, 1)
     woven = lax.dot_general(
-        slab[...].reshape(3 * NX * ROWS, 3 * Z), perm[...], (((1,), (1,)), ((), ())),
+        slab[...].reshape(3 * NX * ROWS_Y, 3 * Z), perm[...], (((1,), (1,)), ((), ())),
         precision=lax.Precision.HIGHEST, preferred_element_type=f32,
-    ).reshape(3, NX, ROWS, 3 * Z)
+    ).reshape(3, NX, ROWS_Y, 3 * Z)
     grad[...] = woven[:, :, 0:NY, :]
     for ix in range(X):
         adv[:, ix] = U[:, ix * Y : ix * Y + Y, :]
-    red_finish(1, 1, jnp.add)
-    every = [RED[1, 2, n] for n in range(groups)]
-
-    def over_all(parts):
-        return sum(jnp.sum(x, axis=1, keepdims=True) for x in parts)
-
-    etot = over_all([x[0:1] for x in every])
-    stot = over_all([x[1:2] for x in every])
+    rows_finish(1)
+    every = [ROWS[1, n] for n in range(devices)]
+    l1 = lax.broadcasted_iota(jnp.int32, (1, Z), 1)
+
+    def lane_sum(x, n):
+        return jnp.sum(jnp.where(l1 == n, x, 0.0), axis=1, keepdims=True)
+
+    sums = sum(x[0:1] for x in every)
+    etot, stot = lane_sum(sums, 0), lane_sum(sums, 1)
     step = trial_step / jnp.sqrt(1.0 + stot / entries)
-    parts = []
-    for n, x in enumerate(every):
-        own = jnp.where(lane[0:1] + n * Z < devices, x[6:7], 1.0)
-        h = step / own
-        parts.append(x[0:1] + h * (x[2:3] + h * (x[3:4] + h * (x[4:5] + h * x[5:6]))))
-    ttot = over_all(parts)
+    higher = jnp.zeros((1, Z), f32)
+    for x in every:
+        h = step * x[1:2]
+        h2 = h * h
+        power = jnp.where(l1 == 2, h2, jnp.where(l1 == 3, h2 * h, h2 * h2))
+        higher = higher + x[0:1] * power
+    higher = jnp.sum(jnp.where((l1 >= 2) & (l1 < 5), higher, 0.0), axis=1, keepdims=True)
+    ttot = (etot - step * stot) + higher
     for ry in range(GY):
         if ry:
             plane_copy(ry).wait_send()
@@ -755,11 +786,8 @@
             cp.wait_send()
     for cp in edge_copies() + edge_core_copies():
         cp.wait_send()
-    for r in range(2):
-        for phase in range(2):
-            for cp in red_copies(r, phase):
-                cp.wait_send()
-    l1 = lax.broadcasted_iota(jnp.int32, (1, Z), 1)
+    rows_sent(0)
+    rows_sent(1)
     checks[...] = jnp.where(
         l1 == 0, etot / elements, jnp.where(l1 == 1, stot / entries, ttot / elements)
     )
@@ -773,8 +801,7 @@
         assert Y == 2 and displacement.shape == (3, 3 * X, 3 * Y, 3 * Z)
         R, NX, NY = 4 * Y, 3 * X, 3 * Y
         tab = jnp.asarray(row_tables(Y, Z))
-        peers = sizes[0] - 1 + sizes[1] * sizes[2] - 1
-        groups = -(-sizes[0] * sizes[1] * sizes[2] // Z)
+        devices = sizes[0] * sizes[1] * sizes[2]
         GX, GY = sizes[0], sizes[1]
         XG, YG, NS = GX * X, GY * Y, GX * X // 2
         packs = -(-30 * X // (Z // (2 * SUBSTEPS)))
@@ -796,12 +823,12 @@
                 vm(27, XG, YG, Z), vm(27, XG, YG, Z), vm(3, XG, YG, Z), vm(XG, 9, YG, Z), vm(XG + 1, 9, YG, Z),
                 vm(27, NS, YG, Z), vm(27, NS, YG, Z), vm(3, NS, YG, Z), vm(NS, 9, YG, Z), vm(NS + 1, 9, YG, Z),
                 vm(3 * Z, 3 * Z), vm(3 * NX, R, 3 * Z), vm(27, R, Z),
-                vm(2, 3, groups, R, Z), vm(2, peers, groups, R, Z),
+                vm(2, devices, 2, Z),
                 vm(3, NX + 1, 4, R, Z), vm(3, NX + 1, 4, R, Z),
                 vm(3, 3, NX + 1, 4, R, Z), vm(3, 3, X, 4, 4, R, Z), vm(3, 3, X, 4, 4, R, Z), vm(2, NX + 1, 4, R, Z), vm(X, 4, 4, R, Z), vm(R, Z),
-                vm(1, 3, 3, R, Z), vm(1, 3, NX + 1, 3, Z), vm(1, 3, NX + 1, 3, Z), vm(1, R, Z), vm(1, R, Z),
-                vm(2, 3, 4, R, Z), vm(2, 3, NX + 1, 4, Z), vm(2, 3, NX + 1, 4, Z), vm(2, R, Z), vm(2, R, Z),
-                dma(3), dma(GY), dma(GY), dma(GX, GY), dma(GX, GY), dma(2, GY), dma(2, GY), dma(GX), dma(GX), dma(2, peers), dma(2, peers), dma(1, 3), dma(1, 3), dma(6), dma(6),
+                vm(3, 3, R, Z), vm(3, NX, 3, Z), vm(3, NX, 3, Z), vm(3, 3, Z), vm(R, Z), vm(4, R, Z),
+                vm(2, 3, 4, R, Z), vm(2, 3, NX + 1, 4, Z), vm(2, 3, NX + 1, 4, Z), vm(2, 2, 3, 4, Z), vm(2, R, Z), vm(2, R, Z), vm(2, 4, 1, Z), vm(2, 8, 1, Z),
+                dma(3), dma(GY), dma(GY), dma(GX, GY), dma(GX, GY), dma(2, GY), dma(2, GY), dma(GX), dma(GX), dma(2, 2), dma(2, 2), dma(7), dma(7), dma(26), dma(26),
             ],
             compiler_params=pltpu.CompilerParams(collective_id=0, has_side_effects=True),
         )(displacement, size_field_modes, velocity, tab)

time: 52 us -> 41.1 us (0.79)
  Pallas kernels: 46.9 us -> 35.9 us
    pallas_call x1, Pallas kernels: 46.9 us -> 35.9 us  [on_device(): pl.pallas_call(functools.partial(kernel, sizes, X, Y, Z), out_shape=(jax....]
where the time goes in v2:
time: 41.1 us; the launch traced here: 40.8 us
  Pallas kernels  35.9 us (87%)
  local copies, waits for them, and re-layouts  4.25 us (10%)
  between operations  0.65 us (2%)
    pallas_call x1, Pallas kernels, on_device(): pl.pallas_call(functools.partial(kernel, sizes, X, Y, Z), out_shape=(jax....  35.9 us
    unnamed x4, local copies, waits for them, and re-layouts  3.74 us

profile of v2, /device:TPU:0, one launch (start us, length us, event | category | flops | bytes accessed | tf_op | source)
XLA Modules:
  0.0 40.8 jit_solution(7256974512768577684)
XLA Ops:
  0.6 35.9 %shard_map.67 = (f32[27,2,2,128]{3,2,1,0:T(2,128)}, f32[3,6,6,384]{3,2,1,0:T(8,128)}, f32[1,128]{1,0:T(1,128)}) custom-call(f32[3,6,6,384]{3,2,1,0:T(8,128)} %disp_in.1, f32[27,2,2,128]{3,2,1,0:T(2,128)} %modes_in.1, f32[3,2,2,128]{3,2,1,0:T(2,128)} %vel_in.1, f32[37,8,128]{2,1,0:T(8,128)} %constant.2.clone.tab), custom_call_target="tpu_custom_call" | custom-call | tf_op jit(solution)/shard_map/pallas_call | solution.py:812
  36.6 0.0 copy-start
  36.6 0.7 %copy-done = f32[1,128]{1,0:T(1,128)S(1)} copy-done((f32[1,128]{1,0:T(1,128)S(1)}, f32[1,128]{1,0:T(1,128)}, u32[]{:S(2)}) %copy-start) | copy-done | bytes 536
  37.2 0.5 %slice_bitcast_fusion = f32[3]{0:T(128)} fusion(f32[1,128]{1,0:T(1,128)S(1)} %copy-done), kind=kLoop, calls=%fused_computation | loop fusion | bytes 24 | tf_op jit(solution)/shard_map/squeeze | solution.py:835
  37.8 1.4 %copy.9 = f32[27,2,2,128]{3,2,1,0:T(2,128)} copy(f32[27,2,2,128]{3,2,1,0:T(2,128)} %get-tuple-element.12) | data formatting | bytes 110592
  39.2 1.6 %copy.10 = f32[3,6,6,384]{3,2,1,0:T(8,128)} copy(f32[3,6,6,384]{3,2,1,0:T(8,128)} %get-tuple-element.13) | data formatting | bytes 331776
Async XLA Ops:
  36.6 0.7 %copy-start = (f32[1,128]{1,0:T(1,128)S(1)}, f32[1,128]{1,0:T(1,128)}, u32[]{:S(2)}) copy-start(f32[1,128]{1,0:T(1,128)} %get-tuple-element.8) | copy-start | bytes 1540

commit v3 on v2

--- a/solution.py
+++ b/solution.py
@@ -793,6 +793,21 @@
     )
 
 
+def publish(adv, grad, checks, adv_out, grad_out, checks_out, sem):
+    copies = [
+        pltpu.make_async_copy(grad, grad_out, sem.at[0]),
+        pltpu.make_async_copy(adv, adv_out, sem.at[1]),
+    ]
+    for cp in copies:
+        cp.start()
+    row = checks[...]
+    lane = lax.broadcasted_iota(jnp.int32, row.shape, 1)
+    for n in range(3):
+        checks_out[n] = jnp.sum(jnp.where(lane == n, row, 0.0))
+    for cp in copies:
+        cp.wait()
+
+
 def solution(mesh):
     sizes = tuple(mesh.shape[a] for a in AXES)
 
@@ -812,9 +827,9 @@
         adv, grad, checks = pl.pallas_call(
             functools.partial(kernel, sizes, X, Y, Z),
             out_shape=(
-                jax.ShapeDtypeStruct(size_field_modes.shape, jnp.float32),
-                jax.ShapeDtypeStruct(displacement.shape, jnp.float32),
-                jax.ShapeDtypeStruct((1, Z), jnp.float32),
+                pltpu.VMEM(size_field_modes.shape, jnp.float32),
+                pltpu.VMEM(displacement.shape, jnp.float32),
+                pltpu.VMEM((1, Z), jnp.float32),
             ),
             in_specs=[pl.BlockSpec(memory_space=pl.ANY)] * 3 + [spec],
             out_specs=(spec,) * 3,
@@ -832,7 +847,19 @@
             ],
             compiler_params=pltpu.CompilerParams(collective_id=0, has_side_effects=True),
         )(displacement, size_field_modes, velocity, tab)
-        return adv, grad, checks[0, 0:3]
+        return tuple(
+            pl.pallas_call(
+                publish,
+                out_shape=(
+                    jax.ShapeDtypeStruct(size_field_modes.shape, jnp.float32),
+                    jax.ShapeDtypeStruct(displacement.shape, jnp.float32),
+                    jax.ShapeDtypeStruct((3,), jnp.float32),
+                ),
+                in_specs=[spec] * 3,
+                out_specs=(pl.BlockSpec(memory_space=pl.ANY),) * 2 + (pl.BlockSpec(memory_space=pltpu.SMEM),),
+                scratch_shapes=[dma(2)],
+            )(*(pltpu.with_memory_space_constraint(a, pltpu.VMEM) for a in (adv, grad, checks)))
+        )
 
     return jax.shard_map(
         on_device,

time: 41.1 us -> 37.3 us (0.908)
  local copies, waits for them, and re-layouts: 4.25 us -> 0 us
  Pallas kernels: 35.9 us -> 36.5 us
    unnamed x4 -> x0, local copies, waits for them, and re-layouts: 3.74 us -> none
    pallas_call x1 -> x2, Pallas kernels: 35.9 us -> 36.5 us  [the longest x1 35.2 us: on_device(): pl.pallas_call(functools.partial(kernel, sizes, X, Y, Z), out_shape=(pltp...]
    squeeze x1 -> x0, local copies, waits for them, and re-layouts: 0.51 us -> none  [on_device(): return (adv, grad, checks[0, 0:3])]
where the time goes in v3:
time: 37.3 us; the launch traced here: 37.1 us
  Pallas kernels  36.5 us (98%)
  between operations  0.64 us (2%)
    pallas_call x1, Pallas kernels, on_device(): pl.pallas_call(functools.partial(kernel, sizes, X, Y, Z), out_shape=(pltp...  35.2 us
    pallas_call x1, Pallas kernels, on_device(): pl.pallas_call(publish, out_shape=(jax.ShapeDtypeStruct(size_field_modes....  1.23 us

profile of v3, /device:TPU:0, one launch (start us, length us, event | category | flops | bytes accessed | tf_op | source)
XLA Modules:
  0.0 37.1 jit_solution(11546973688983039119)
XLA Ops:
  0.6 35.2 %shard_map.67 = (f32[27,2,2,128]{3,2,1,0:T(2,128)S(1)}, f32[3,6,6,384]{3,2,1,0:T(8,128)S(1)}, f32[1,128]{1,0:T(1,128)S(1)}) custom-call(f32[3,6,6,384]{3,2,1,0:T(8,128)} %disp_in.1, f32[27,2,2,128]{3,2,1,0:T(2,128)} %modes_in.1, f32[3,2,2,128]{3,2,1,0:T(2,128)} %vel_in.1, f32[37,8,128]{2,1,0:T(8,128)} %constant.2.clone.tab), custom_call_target="tpu_custom_call" | custom-call | tf_op jit(solution)/shard_map/pallas_call | solution.py:827
  35.9 1.2 %shard_map.68 = (f32[27,2,2,128]{3,2,1,0:T(2,128)}, f32[3,6,6,384]{3,2,1,0:T(8,128)}, f32[3]{0:T(128)}) custom-call(f32[27,2,2,128]{3,2,1,0:T(2,128)S(1)} %get-tuple-element.6.adv, f32[3,6,6,384]{3,2,1,0:T(8,128)S(1)} %get-tuple-element.7.grad, f32[1,128]{1,0:T(1,128)S(1)} %get-tuple-element.8.checks), custom_call_target="tpu_custom_call" | custom-call | tf_op jit(solution)/shard_map/pallas_call | solution.py:851

commit v4 on v3

--- a/solution.py
+++ b/solution.py
@@ -73,8 +73,8 @@
     return np.ascontiguousarray(np.broadcast_to(stacked[:, :, None], stacked.shape + (Z,)))
 
 
-def kernel(sizes, X, Y, Z, disp_in, modes_in, vel_in, tab, adv, grad, checks,
-           disp, GU, ZP, ZR, ZA, UM, WM, VM, CM, FM, US, WS, VS, CS, FT,
+def kernel(sizes, X, Y, Z, disp_in, modes_in, vel_in, tab_in, adv, grad, checks,
+           disp, tab, GU, ZP, ZR, ZA, UM, VM, CM, FM, US, VS, CS, FT,
            perm, slab, U, ROWS, N, GN, A, G, J, B, SIZ, DT,
            NXR, NYS, NYR, NXYR, NZS, NZR, FXR, FYS, FYR, FXYR, FZS, FZR, FES, FER,
            ls, g1s, g1r, g2s, g2r, zs, zr, y2s, y2r, rs, rr, ns, nr, fs, fr):
@@ -92,20 +92,13 @@
         n = sizes[axis]
         return {AXES[axis]: lax.rem(index[axis] + (by + n), n)}
 
-    loads = [
-        pltpu.make_async_copy(modes_in, GU.at[0, 0, 0:27], ls.at[0]),
-        pltpu.make_async_copy(vel_in, GU.at[0, 0, 27:30], ls.at[1]),
-        pltpu.make_async_copy(disp_in, disp, ls.at[2]),
-    ]
-    for cp in loads:
-        cp.start()
     barrier = pltpu.get_barrier_semaphore()
     total = 0
     for a in range(sizes[0]):
         for b in range(sizes[1]):
             for c in range(sizes[2]):
                 move = (a, b, c)
-                if not any(move):
+                if not any(move) or (c and (a or b)):
                     continue
                 target = {}
                 for axis in range(3):
@@ -114,6 +107,15 @@
                 pl.semaphore_signal(barrier, inc=1, device_id=target, device_id_type=MESH)
                 total += 1
 
+    loads = [
+        pltpu.make_async_copy(modes_in, GU.at[0, 0, 0:27], ls.at[0]),
+        pltpu.make_async_copy(vel_in, GU.at[0, 0, 27:30], ls.at[1]),
+        pltpu.make_async_copy(disp_in, disp, ls.at[2]),
+        pltpu.make_async_copy(tab_in, tab, ls.at[3]),
+    ]
+    for cp in loads:
+        cp.start()
+
     def copy(src, dst, ss, sr, axis, by):
         return pltpu.make_async_remote_copy(
             src_ref=src, dst_ref=dst, send_sem=ss, recv_sem=sr,
@@ -148,8 +150,13 @@
 
     def edge_copies():
         return [
-            remote(ZP.at[side], ZR.at[0, ry, side], zs.at[side, ry], zr.at[side, ry], (0, -ry, 2 * side - 1))
-            for side in range(2) for ry in range(GY)
+            remote(ZP.at[side], ZR.at[0, 0, side], zs.at[side, 0], zr.at[side, 0], (0, 0, 2 * side - 1))
+            for side in range(2)
+        ]
+
+    def edge_plane_copies():
+        return [
+            remote(ZR.at[0, 0], ZR.at[0, ry], zs.at[0, ry], zr.at[0, ry], (0, -ry, 0)) for ry in range(1, GY)
         ]
 
     def edge_core_copies():
@@ -174,15 +181,6 @@
         for side in range(2):
             for v in range(packs):
                 ZP[side, v] = acc[side][v]
-
-    for cp in loads[:2]:
-        cp.wait()
-    speed = None
-    for ix in range(X):
-        here = jnp.abs(GU[0, 0, 27, ix]) + jnp.abs(GU[0, 0, 28, ix]) + jnp.abs(GU[0, 0, 29, ix])
-        speed = here if speed is None else jnp.maximum(speed, here)
-    ROWS[0, 0] = jnp.broadcast_to(jnp.max(speed, axis=0, keepdims=True), (2, Z))
-    pack_edges()
 
     def unweave():
         a_i = lax.broadcasted_iota(jnp.int32, (3 * Z, 3 * Z), 0)
@@ -201,21 +199,13 @@
             for k in range(3):
                 N[c, 0:NX, k] = spread[c, :, :, k * Z : (k + 1) * Z]
 
-    loads[2].wait()
-    unweave()
-    pl.semaphore_wait(barrier, total)
-    for cp in core_copies(0):
-        cp.start()
-    for ry in range(1, GY):
-        plane_copy(ry).start()
-    for cp in edge_copies():
-        cp.start()
-
     devices = sizes[0] * sizes[1] * sizes[2]
-    stages = [(0, 1, 2)] if devices <= 64 else [(0,), (1, 2)]
+    by_column = [(2,), (0, 1)]
+    plans = [by_column, [(0, 1, 2)] if devices <= 64 else by_column]
 
     def row_stage(r, stage):
         block = 1
+        stages = plans[r]
         for axes in stages[:stage]:
             for axis in axes:
                 block *= sizes[axis]
@@ -234,14 +224,16 @@
         for cp in row_stage(r, stage)[0]:
             cp.start()
 
+    def rows_relay(r):
+        for stage in range(len(plans[r]) - 1):
+            row_stage(r, stage)[1].wait_recv()
+            rows_start(r, stage + 1)
+
     def rows_finish(r):
-        for stage in range(len(stages)):
-            row_stage(r, stage)[1].wait_recv()
-            if stage + 1 < len(stages):
-                rows_start(r, stage + 1)
+        row_stage(r, len(plans[r]) - 1)[1].wait_recv()
 
     def rows_sent(r):
-        for stage in range(len(stages)):
+        for stage in range(len(plans[r])):
             row_stage(r, stage)[1].wait_send()
 
     in_lane = lambda n: functools.reduce(jnp.logical_or, [lane == c * (NX + 1) + n for c in range(3)])
@@ -252,9 +244,16 @@
             remote(NYS, NYR, ns.at[1], nr.at[1], (0, -1, 0)),
             remote(NYS.at[:, 0], NXYR, ns.at[2], nr.at[2], (-1, -1, 0)),
         ]
-        for n, move in enumerate(((0, 0, -1), (-1, 0, -1), (0, -1, -1), (-1, -1, -1))):
-            out.append(remote(NZS, NZR.at[n], ns.at[3 + n], nr.at[3 + n], move))
         return out
+
+    def rim_column():
+        return remote(NZS, NZR.at[0], ns.at[3], nr.at[3], (0, 0, -1))
+
+    def rim_relays():
+        return [
+            remote(NZR.at[0], NZR.at[n], ns.at[3 + n], nr.at[3 + n], move)
+            for n, move in ((1, (-1, 0, 0)), (2, (0, -1, 0)), (3, (-1, -1, 0)))
+        ]
 
     def rim_pack():
         packed = jnp.zeros((ROWS_Y, Z), f32)
@@ -272,14 +271,27 @@
                 N[c, NX, k, NY : NY + 1, :] = NXYR[c, k : k + 1, :]
                 for i in range(NX):
                     N[c, i, k, NY : NY + 1, :] = NYR[c, i, k : k + 1, :]
+        for c in range(3):
+            for i in range(NX + 1):
+                N[c, i, 3] = jnp.where(lane == Z - 1, 0.0, pltpu.roll(N[c, i, 0], Z - 1, 1))
+
+    def rim_last():
         last = in_lane(NX)
         packed = jnp.where(last, pltpu.roll(NZR[1], NX, 1), NZR[0])
         below = jnp.where(last[0:1], pltpu.roll(NZR[3], NX, 1)[0:1], NZR[2][0:1])
-        packed = jnp.where(row == NY, jnp.broadcast_to(below, (ROWS_Y, Z)), packed)
+        rows = [packed[j : j + 1] for j in range(NY)] + [below]
+        pv = sum(tab[oTV + j] * rows[j] for j in range(NY + 1))
+        pd = sum(tab[oTD + j] * rows[j] for j in range(NY + 1))
+        end = lane == Z - 1
         for c in range(3):
             for i in range(NX + 1):
-                at_ = c * (NX + 1) + i
-                N[c, i, 3] = jnp.where(lane == Z - 1, packed[:, at_ : at_ + 1], pltpu.roll(N[c, i, 0], Z - 1, 1))
+                n = c * (NX + 1) + i
+                mv = jnp.where(end, pv[:, n : n + 1], 0.0)
+                md = jnp.where(end, pd[:, n : n + 1], 0.0)
+                for r in range(4):
+                    A[0, c, i, r] = A[0, c, i, r] + float(value[r, 3]) * mv
+                    A[1, c, i, r] = A[1, c, i, r] + float(value[r, 3]) * md
+                    A[2, c, i, r] = A[2, c, i, r] + float(slope[r, 3]) * mv
 
     scale = [plus_values[m // 9] * plus_values[m // 3 % 3] * plus_values[m % 3] for m in range(27)]
 
@@ -290,7 +302,7 @@
                 for m in range(FIELDS):
                     v = GU[rx, ry, m, ix]
                     if m < 27:
-                        UM[m, x, ry * Y : ry * Y + Y, :] = scale[m] * v
+                        UM[0, m, x, ry * Y : ry * Y + Y, :] = scale[m] * v
                     else:
                         VM[m - 27, x, ry * Y : ry * Y + Y, :] = v
             return carry
@@ -308,12 +320,12 @@
             for m in range(FIELDS):
                 out = jnp.zeros((YG, Z), f32)
                 for h in range(2):
-                    t = UM[m, q + h * NS] if m < 27 else VM[m - 27, q + h * NS]
+                    t = UM[0, m, q + h * NS] if m < 27 else VM[m - 27, q + h * NS]
                     o = h * HALF
                     out = jnp.where(within(o, o + W2), pltpu.roll(t, o + W2, 1), out)
                     out = jnp.where(within(o + 2 * W2, o + 3 * W2), pltpu.roll(t, o + 2 * W2, 1), out)
                 if m < 27:
-                    US[m, q] = out
+                    US[0, m, q] = out
                 else:
                     VS[m - 27, q] = out
             return carry
@@ -326,7 +338,7 @@
                 ZA[rx, :, :, ry * Y : ry * Y + Y, :] = ZR[rx, ry]
         for q in range(NS):
             for m in range(FIELDS):
-                out = US[m, q] if m < 27 else VS[m - 27, q]
+                out = US[0, m, q] if m < 27 else VS[m - 27, q]
                 for h in range(2):
                     x = q + h * NS
                     rx, ix = x // X, x % X
@@ -341,7 +353,7 @@
                             piece = scale[m] * piece
                         out = jnp.where(within(o, o + EDGE), piece, out)
                 if m < 27:
-                    US[m, q] = out
+                    US[0, m, q] = out
                 else:
                     VS[m - 27, q] = out
 
@@ -358,16 +370,15 @@
         return pltpu.roll(t, 1, 1)
 
     def coefficients(V, C, nx, wrap):
-        dt = DT[...]
         for q in range(nx):
             nxt = V[0, q + 1] if q < nx - 1 else wrap(V[0, 0])
             for d in range(3):
                 v = V[d, q]
                 ahead = nxt if d == 0 else ynext(v) if d == 1 else znext(v)
-                face = (0.5 * dt) * (v + ahead)
+                face = 0.5 * (v + ahead)
                 C[q, 3 * d] = jnp.maximum(face, 0.0)
                 C[q, 3 * d + 1] = jnp.minimum(face, 0.0)
-                C[q, 3 * d + 2] = (2.0 * dt) * v
+                C[q, 3 * d + 2] = 2.0 * v
 
     def line(u, hp, hm, v2, ahead, behind):
         e = u[0] + u[2]
@@ -376,7 +387,7 @@
         diff = low - up
         return diff, 3.0 * (v2 * u[0] - (low + up)), 5.0 * (v2 * u[1] + diff)
 
-    def rate(src, C, F, nx, wrap, write):
+    def rate(src, dst, C, F, nx, wrap):
         for n in range(9):
             tp, tm = [], []
             for q in range(nx):
@@ -412,7 +423,7 @@
                         for t in range(3):
                             acc[at_[t]] = acc[at_[t]] + out[t]
                 for n in range(9):
-                    write(9 * a + n, q, acc[n])
+                    dst[9 * a + n, q] = acc[n]
             return carry
 
         if nx <= 4:
@@ -421,19 +432,12 @@
         else:
             lax.fori_loop(0, nx, block, 0)
 
-    def advance(Ur, Wr, C, F, nx, wrap):
-        def put(m, q, value):
-            Wr[m, q] = value
-
-        def step(m, q, value):
-            Ur[m, q] = (Ur[m, q] + Wr[m, q]) + 0.5 * value
-
-        def substep(t, carry):
-            rate(Ur, C, F, nx, wrap, put)
-            rate(Wr, C, F, nx, wrap, step)
+    def powers(P, C, F, nx, wrap, first, last):
+        def one(k, carry):
+            rate(P.at[k], P.at[k + 1], C, F, nx, wrap)
             return carry
 
-        lax.fori_loop(0, SUBSTEPS, substep, 0)
+        lax.fori_loop(first, last, one, 0)
 
     def same(t):
         return t
@@ -441,13 +445,26 @@
     def half_turn(t):
         return pltpu.roll(t, HALF, 1)
 
+    taylor = np.polynomial.polynomial.polypow([1.0, 1.0, 0.5], SUBSTEPS)
+
     def finish_field():
         U[...] = jnp.zeros_like(U)
+        dt = DT[...]
+        weight, power = [], None
+        for k in range(1, 2 * SUBSTEPS + 1):
+            power = dt if power is None else power * dt
+            weight.append(float(taylor[k]) * power)
+
+        def summed(P, m, q):
+            out = P[0, m, q]
+            for k in range(1, 2 * SUBSTEPS + 1):
+                out = out + weight[k - 1] * P[k, m, q]
+            return out
+
         for m in range(27):
             for ix in range(X):
-                t = UM[m, ix]
                 h, q = ix // NS, ix % NS
-                s = US[m, q]
+                t, s = summed(UM, m, ix), summed(US, m, q)
                 o = h * HALF
                 left = pltpu.roll(s, (Z - o - 2 * W2) % Z, 1)
                 right = pltpu.roll(s, (Z - W2 - o) % Z, 1)
@@ -487,44 +504,74 @@
                     jac = slope_at(ix, p, r, c, d)
                     J[d, c, ix, p, r] = jac + 1.0 if c == d else jac
 
+    for cp in loads[:2]:
+        cp.wait()
+    pl.semaphore_wait(barrier, total)
+    for cp in core_copies(0):
+        cp.start()
+    for ry in range(1, GY):
+        plane_copy(ry).start()
+    speed = None
+    for ix in range(X):
+        here = jnp.abs(GU[0, 0, 27, ix]) + jnp.abs(GU[0, 0, 28, ix]) + jnp.abs(GU[0, 0, 29, ix])
+        speed = here if speed is None else jnp.maximum(speed, here)
+    ROWS[0, 0] = jnp.broadcast_to(jnp.max(speed, axis=0, keepdims=True), (2, Z))
     rows_start(0, 0)
+    pack_edges()
+    for cp in edge_copies():
+        cp.start()
+    loads[2].wait()
+    unweave()
     rim_pack()
+    rim_column().start()
     for cp in rim_copies():
+        cp.start()
+    loads[3].wait()
+    for cp in edge_copies():
+        cp.wait_recv()
+    for cp in edge_plane_copies():
         cp.start()
     for ry in range(1, GY):
         plane_copy(ry).wait_recv()
         for cp in core_copies(ry):
             cp.start()
-    for cp in edge_copies():
-        cp.wait_recv()
-    for cp in edge_core_copies():
+    rows_relay(0)
+    rim_column().wait_recv()
+    for cp in rim_relays():
         cp.start()
     for cp in rim_copies():
         cp.wait()
     rim_unpack()
     yz_of(N)
-
-    def all_jacobians(t, carry):
-        jacobians(t)
-        return carry
-
-    lax.fori_loop(0, 4 * X, all_jacobians, 0)
-    rows_finish(0)
-    fastest = functools.reduce(jnp.maximum, [ROWS[0, n] for n in range(devices)])
-    fastest = jnp.max(fastest, axis=(0, 1), keepdims=True)
-    DT[...] = jnp.broadcast_to(courant / jnp.maximum(fastest, 0.25), (YG, Z))
     for ry in range(GY):
         for cp in core_copies(ry):
             cp.wait_recv()
     assemble()
     strip_own()
     coefficients(VM, CM, XG, same)
-    advance(UM, WM, CM, FM, XG, same)
+    for cp in edge_plane_copies():
+        cp.wait_recv()
+    for cp in edge_core_copies():
+        cp.start()
+    powers(UM, CM, FM, XG, same, 0, 2 * SUBSTEPS)
+    for cp in rim_relays():
+        cp.wait_recv()
+    rim_last()
+
+    def all_jacobians(t, carry):
+        jacobians(t)
+        return carry
+
+    lax.fori_loop(0, 4 * X, all_jacobians, 0)
     for cp in edge_core_copies():
         cp.wait_recv()
     strip_halo()
     coefficients(VS, CS, NS, half_turn)
-    advance(US, WS, CS, FT, NS, half_turn)
+    powers(US, CS, FT, NS, half_turn, 0, 2 * SUBSTEPS)
+    rows_finish(0)
+    fastest = functools.reduce(jnp.maximum, [ROWS[0, n] for n in range(devices)])
+    fastest = jnp.max(fastest, axis=(0, 1), keepdims=True)
+    DT[...] = jnp.broadcast_to(courant / jnp.maximum(fastest, 0.25), (YG, Z))
     finish_field()
     def size_of(ix, carry):
         mid = {}
@@ -761,6 +808,7 @@
     grad[...] = woven[:, :, 0:NY, :]
     for ix in range(X):
         adv[:, ix] = U[:, ix * Y : ix * Y + Y, :]
+    rows_relay(1)
     rows_finish(1)
     every = [ROWS[1, n] for n in range(devices)]
     l1 = lax.broadcasted_iota(jnp.int32, (1, Z), 1)
@@ -784,7 +832,7 @@
             plane_copy(ry).wait_send()
         for cp in core_copies(ry):
             cp.wait_send()
-    for cp in edge_copies() + edge_core_copies():
+    for cp in edge_copies() + edge_plane_copies() + edge_core_copies() + [rim_column()] + rim_relays():
         cp.wait_send()
     rows_sent(0)
     rows_sent(1)
@@ -831,19 +879,19 @@
                 pltpu.VMEM(displacement.shape, jnp.float32),
                 pltpu.VMEM((1, Z), jnp.float32),
             ),
-            in_specs=[pl.BlockSpec(memory_space=pl.ANY)] * 3 + [spec],
+            in_specs=[pl.BlockSpec(memory_space=pl.ANY)] * 4,
             out_specs=(spec,) * 3,
             scratch_shapes=[
-                vm(3, NX, NY, 3 * Z), vm(GX, GY, 30, X, Y, Z), vm(2, packs, Y, Z), vm(GX, GY, 2, packs, Y, Z), vm(GX, 2, packs, YG, Z),
-                vm(27, XG, YG, Z), vm(27, XG, YG, Z), vm(3, XG, YG, Z), vm(XG, 9, YG, Z), vm(XG + 1, 9, YG, Z),
-                vm(27, NS, YG, Z), vm(27, NS, YG, Z), vm(3, NS, YG, Z), vm(NS, 9, YG, Z), vm(NS + 1, 9, YG, Z),
+                vm(3, NX, NY, 3 * Z), vm(*tab.shape), vm(GX, GY, 30, X, Y, Z), vm(2, packs, Y, Z), vm(GX, GY, 2, packs, Y, Z), vm(GX, 2, packs, YG, Z),
+                vm(2 * SUBSTEPS + 1, 27, XG, YG, Z), vm(3, XG, YG, Z), vm(XG, 9, YG, Z), vm(XG + 1, 9, YG, Z),
+                vm(2 * SUBSTEPS + 1, 27, NS, YG, Z), vm(3, NS, YG, Z), vm(NS, 9, YG, Z), vm(NS + 1, 9, YG, Z),
                 vm(3 * Z, 3 * Z), vm(3 * NX, R, 3 * Z), vm(27, R, Z),
                 vm(2, devices, 2, Z),
                 vm(3, NX + 1, 4, R, Z), vm(3, NX + 1, 4, R, Z),
                 vm(3, 3, NX + 1, 4, R, Z), vm(3, 3, X, 4, 4, R, Z), vm(3, 3, X, 4, 4, R, Z), vm(2, NX + 1, 4, R, Z), vm(X, 4, 4, R, Z), vm(R, Z),
                 vm(3, 3, R, Z), vm(3, NX, 3, Z), vm(3, NX, 3, Z), vm(3, 3, Z), vm(R, Z), vm(4, R, Z),
                 vm(2, 3, 4, R, Z), vm(2, 3, NX + 1, 4, Z), vm(2, 3, NX + 1, 4, Z), vm(2, 2, 3, 4, Z), vm(2, R, Z), vm(2, R, Z), vm(2, 4, 1, Z), vm(2, 8, 1, Z),
-                dma(3), dma(GY), dma(GY), dma(GX, GY), dma(GX, GY), dma(2, GY), dma(2, GY), dma(GX), dma(GX), dma(2, 2), dma(2, 2), dma(7), dma(7), dma(26), dma(26),
+                dma(4), dma(GY), dma(GY), dma(GX, GY), dma(GX, GY), dma(2, GY), dma(2, GY), dma(GX), dma(GX), dma(2, 2), dma(2, 2), dma(7), dma(7), dma(26), dma(26),
             ],
             compiler_params=pltpu.CompilerParams(collective_id=0, has_side_effects=True),
         )(displacement, size_field_modes, velocity, tab)

time: 37.3 us -> 35.4 us (0.949)
  Pallas kernels: 36.5 us -> 34.6 us
    pallas_call x1, Pallas kernels: 35.2 us -> 33.4 us  [on_device(): pl.pallas_call(functools.partial(kernel, sizes, X, Y, Z), out_shape=(pltp...]
where the time goes in v4:
time: 35.4 us; the launch traced here: 35.3 us
  Pallas kernels  34.6 us (98%)
  between operations  0.64 us (2%)
    pallas_call x1, Pallas kernels, on_device(): pl.pallas_call(functools.partial(kernel, sizes, X, Y, Z), out_shape=(pltp...  33.4 us
    pallas_call x1, Pallas kernels, on_device(): pl.pallas_call(publish, out_shape=(jax.ShapeDtypeStruct(size_field_modes....  1.23 us

profile of v4, /device:TPU:0, one launch (start us, length us, event | category | flops | bytes accessed | tf_op | source)
XLA Modules:
  0.0 35.3 jit_solution(11044658005895755366)
XLA Ops:
  0.6 33.4 %shard_map.67 = (f32[27,2,2,128]{3,2,1,0:T(2,128)S(1)}, f32[3,6,6,384]{3,2,1,0:T(8,128)S(1)}, f32[1,128]{1,0:T(1,128)S(1)}) custom-call(f32[3,6,6,384]{3,2,1,0:T(8,128)} %disp_in.1, f32[27,2,2,128]{3,2,1,0:T(2,128)} %modes_in.1, f32[3,2,2,128]{3,2,1,0:T(2,128)} %vel_in.1, f32[37,8,128]{2,1,0:T(8,128)} %constant.2.clone.tab_in), custom_call_target="tpu_custom_call" | custom-call | tf_op jit(solution)/shard_map/pallas_call | solution.py:875
  34.0 1.2 %shard_map.68 = (f32[27,2,2,128]{3,2,1,0:T(2,128)}, f32[3,6,6,384]{3,2,1,0:T(8,128)}, f32[3]{0:T(128)}) custom-call(f32[27,2,2,128]{3,2,1,0:T(2,128)S(1)} %get-tuple-element.6.adv, f32[3,6,6,384]{3,2,1,0:T(8,128)S(1)} %get-tuple-element.7.grad, f32[1,128]{1,0:T(1,128)S(1)} %get-tuple-element.8.checks), custom_call_target="tpu_custom_call" | custom-call | tf_op jit(solution)/shard_map/pallas_call | solution.py:899

commit v5 on v4

--- a/solution.py
+++ b/solution.py
@@ -215,7 +215,7 @@
         src = ROWS.at[r, 0:block]
         copies = [
             remote(src, ROWS.at[r, n * block : (n + 1) * block], rs.at[r, stage], rr.at[r, stage], m)
-            for n, m in enumerate(moves) if n
+            for n, m in sorted(enumerate(moves), key=lambda nm: -sum(1 for b in nm[1] if b)) if n
         ]
         rest = ROWS.at[r, block : len(moves) * block]
         return copies, remote(rest, rest, rs.at[r, stage], rr.at[r, stage], moves[1])
@@ -492,17 +492,27 @@
 
         lax.fori_loop(0, NX + 1, yz, 0)
 
-    def slope_at(ix, p, r, c, d):
+    def slopes_at(ix, r, c, d):
         tb = slope if d == 0 else value
-        return sum(float(tb[p, m]) * A[d, c, 3 * ix + m, r] for m in range(4))
+        x = [A[d, c, 3 * ix + m, r] for m in range(4)]
+        e0, e1, o0, o1 = x[0] + x[3], x[1] + x[2], x[0] - x[3], x[1] - x[2]
+        even = lambda p, m: float(0.5 * (tb[p, m] + tb[p, 3 - m]))
+        odd = lambda p, m: float(0.5 * (tb[p, m] - tb[p, 3 - m]))
+        out = [None] * 4
+        for p in range(2):
+            a = even(p, 0) * e0 + even(p, 1) * e1
+            b = odd(p, 0) * o0 + odd(p, 1) * o1
+            out[p] = a + b
+            out[3 - p] = b - a if d == 0 else a - b
+        return out
 
     def jacobians(t):
         ix, r = t // 4, t % 4
-        for p in range(4):
-            for c in range(3):
-                for d in range(3):
-                    jac = slope_at(ix, p, r, c, d)
-                    J[d, c, ix, p, r] = jac + 1.0 if c == d else jac
+        for c in range(3):
+            for d in range(3):
+                jac = slopes_at(ix, r, c, d)
+                for p in range(4):
+                    J[d, c, ix, p, r] = jac[p] + 1.0 if c == d else jac[p]
 
     for cp in loads[:2]:
         cp.wait()
@@ -515,7 +525,7 @@
     for ix in range(X):
         here = jnp.abs(GU[0, 0, 27, ix]) + jnp.abs(GU[0, 0, 28, ix]) + jnp.abs(GU[0, 0, 29, ix])
         speed = here if speed is None else jnp.maximum(speed, here)
-    ROWS[0, 0] = jnp.broadcast_to(jnp.max(speed, axis=0, keepdims=True), (2, Z))
+    ROWS[0, 0] = jnp.max(speed, axis=0, keepdims=True)
     rows_start(0, 0)
     pack_edges()
     for cp in edge_copies():
@@ -736,26 +746,27 @@
                 col = jnp.sum(jnp.where(lane == c * ROWS_Y + row, edge, 0.0), axis=1, keepdims=True)
                 p = p + jnp.where(lane == c * (NX + 1) + i, col, 0.0)
         planes.append(p)
+    first_row, last_row = row == 0, row == NY
+    ssum = zero
     for c in range(3):
-        for k in range(4):
-            for xs_, i in enumerate((0, NX)):
-                GN[c, i, k] = GN[c, i, k] + FXR[xs_, c, k]
-                for ys_, j in enumerate((0, NY)):
-                    GN[c, i, k, j : j + 1, :] = GN[c, i, k, j : j + 1, :] + FXYR[xs_, ys_, c, k : k + 1, :]
-            for i in range(NX + 1):
-                for ys_, j in enumerate((0, NY)):
-                    GN[c, i, k, j : j + 1, :] = GN[c, i, k, j : j + 1, :] + FYR[ys_, c, i, k : k + 1, :]
         for i in range(NX + 1):
             n = c * (NX + 1) + i
-            full = GN[c, i, 0] + jnp.where(lane == 0, planes[0][:, n : n + 1], 0.0)
-            GN[c, i, 0] = full
-            GN[c, i, 3] = jnp.where(lane == Z - 1, GN[c, i, 3] + planes[1][:, n : n + 1], pltpu.roll(full, Z - 1, 1))
-    ssum = zero
-    for c in range(3):
-        for i in range(NX):
-            for k in range(3):
+            out = []
+            for k in range(4):
+                low, high = FYR[0, c, i, k : k + 1, :], FYR[1, c, i, k : k + 1, :]
                 g = GN[c, i, k]
-                ssum = ssum + g * g
+                if i in (0, NX):
+                    xs_ = 0 if i == 0 else 1
+                    g = g + FXR[xs_, c, k]
+                    low = low + FXYR[xs_, 0, c, k : k + 1, :]
+                    high = high + FXYR[xs_, 1, c, k : k + 1, :]
+                out.append(g + jnp.where(first_row, low, jnp.where(last_row, high, 0.0)))
+            out[0] = out[0] + jnp.where(lane == 0, planes[0][:, n : n + 1], 0.0)
+            out[3] = jnp.where(lane == Z - 1, out[3] + planes[1][:, n : n + 1], pltpu.roll(out[0], Z - 1, 1))
+            for k in range(4):
+                GN[c, i, k] = out[k]
+                if i < NX and k < 3:
+                    ssum = ssum + out[k] * out[k]
     ssum = jnp.where(row < NY, ssum, 0.0)
     elements = float(EL * Z * devices)
     entries = 81.0 * elements
@@ -767,14 +778,15 @@
     def trial(t, sums):
         ix, r = t // 4, t % 4
         s2, s3, s4 = sums
+        moves = [[slopes_at(ix, r, c, d) for d in range(3)] for c in range(3)]
         for p in range(4):
             size = SIZ[ix, p, r]
             inv = 1.0 / size
             move = -(inv * bound)
             M = [[J[d, c, ix, p, r] * inv for d in range(3)] for c in range(3)]
-            K = [[slope_at(ix, p, r, c, d) * move for d in range(3)] for c in range(3)]
+            K = [[moves[c][d][p] * move for d in range(3)] for c in range(3)]
             w = wrow * (gauss_weight(r) * float(weights[p])) * (size * size * size)
-            q = [None] * 3
+            q = [[None] * 4, [None] * 4]
             for d, e in pairs:
                 d0 = dot3(M, M, d, e)
                 d2 = dot3(K, K, d, e)
@@ -783,11 +795,13 @@
                     d1 = 2.0 * dot3(M, K, d, d)
                 else:
                     d1 = dot3(M, K, d, e) + dot3(K, M, d, e)
-                terms = [d1 * d1 + 2.0 * (d0 * d2), 2.0 * (d1 * d2), d2 * d2]
-                for n in range(3):
-                    term = terms[n] if d == e else 2.0 * terms[n]
-                    q[n] = term if q[n] is None else q[n] + term
-            s2, s3, s4 = s2 + w * q[0], s3 + w * q[1], s4 + w * q[2]
+                terms, own = (d1 * d1, d0 * d2, d1 * d2, d2 * d2), q[0 if d == e else 1]
+                for n in range(4):
+                    own[n] = terms[n] if own[n] is None else own[n] + terms[n]
+            full = [q[0][n] + 2.0 * q[1][n] for n in range(4)]
+            s2 = s2 + w * (full[0] + 2.0 * full[1])
+            s3 = s3 + w * (2.0 * full[2])
+            s4 = s4 + w * full[3]
         return s2, s3, s4
 
     sums = lax.fori_loop(0, 4 * X, trial, (zero,) * 3)
@@ -795,8 +809,8 @@
     for n, part in enumerate((esum, ssum) + tuple(sums)):
         block = jnp.where(row == n, jnp.sum(part, axis=0, keepdims=True), block)
     column = jnp.sum(block, axis=1, keepdims=True)
-    ROWS[1, 0, 0:1] = jnp.sum(jnp.where(lane == row, column, 0.0), axis=0, keepdims=True)
-    ROWS[1, 0, 1:2] = 1.0 / bound[0:1]
+    sent = jnp.sum(jnp.where(lane == row, column, 0.0), axis=0, keepdims=True)
+    ROWS[1, 0] = jnp.where(lane[0:1] < HALF, sent, 1.0 / bound[0:1])
     rows_start(1, 0)
     for c in range(3):
         for k in range(3):
@@ -808,25 +822,6 @@
     grad[...] = woven[:, :, 0:NY, :]
     for ix in range(X):
         adv[:, ix] = U[:, ix * Y : ix * Y + Y, :]
-    rows_relay(1)
-    rows_finish(1)
-    every = [ROWS[1, n] for n in range(devices)]
-    l1 = lax.broadcasted_iota(jnp.int32, (1, Z), 1)
-
-    def lane_sum(x, n):
-        return jnp.sum(jnp.where(l1 == n, x, 0.0), axis=1, keepdims=True)
-
-    sums = sum(x[0:1] for x in every)
-    etot, stot = lane_sum(sums, 0), lane_sum(sums, 1)
-    step = trial_step / jnp.sqrt(1.0 + stot / entries)
-    higher = jnp.zeros((1, Z), f32)
-    for x in every:
-        h = step * x[1:2]
-        h2 = h * h
-        power = jnp.where(l1 == 2, h2, jnp.where(l1 == 3, h2 * h, h2 * h2))
-        higher = higher + x[0:1] * power
-    higher = jnp.sum(jnp.where((l1 >= 2) & (l1 < 5), higher, 0.0), axis=1, keepdims=True)
-    ttot = (etot - step * stot) + higher
     for ry in range(GY):
         if ry:
             plane_copy(ry).wait_send()
@@ -836,6 +831,25 @@
         cp.wait_send()
     rows_sent(0)
     rows_sent(1)
+    rows_relay(1)
+    rows_finish(1)
+    every = [ROWS[1, n] for n in range(devices)]
+    l1 = lax.broadcasted_iota(jnp.int32, (1, Z), 1)
+
+    def lane_sum(x, n):
+        return jnp.sum(jnp.where(l1 == n, x, 0.0), axis=1, keepdims=True)
+
+    sums = sum(every)
+    etot, stot = lane_sum(sums, 0), lane_sum(sums, 1)
+    step = trial_step / jnp.sqrt(1.0 + stot / entries)
+    higher = jnp.zeros((1, Z), f32)
+    for x in every:
+        h = step * pltpu.roll(x, HALF, 1)
+        h2 = h * h
+        power = jnp.where(l1 == 2, h2, jnp.where(l1 == 3, h2 * h, h2 * h2))
+        higher = higher + x * power
+    higher = jnp.sum(jnp.where((l1 >= 2) & (l1 < 5), higher, 0.0), axis=1, keepdims=True)
+    ttot = (etot - step * stot) + higher
     checks[...] = jnp.where(
         l1 == 0, etot / elements, jnp.where(l1 == 1, stot / entries, ttot / elements)
     )
@@ -886,7 +900,7 @@
                 vm(2 * SUBSTEPS + 1, 27, XG, YG, Z), vm(3, XG, YG, Z), vm(XG, 9, YG, Z), vm(XG + 1, 9, YG, Z),
                 vm(2 * SUBSTEPS + 1, 27, NS, YG, Z), vm(3, NS, YG, Z), vm(NS, 9, YG, Z), vm(NS + 1, 9, YG, Z),
                 vm(3 * Z, 3 * Z), vm(3 * NX, R, 3 * Z), vm(27, R, Z),
-                vm(2, devices, 2, Z),
+                vm(2, devices, 1, Z),
                 vm(3, NX + 1, 4, R, Z), vm(3, NX + 1, 4, R, Z),
                 vm(3, 3, NX + 1, 4, R, Z), vm(3, 3, X, 4, 4, R, Z), vm(3, 3, X, 4, 4, R, Z), vm(2, NX + 1, 4, R, Z), vm(X, 4, 4, R, Z), vm(R, Z),
                 vm(3, 3, R, Z), vm(3, NX, 3, Z), vm(3, NX, 3, Z), vm(3, 3, Z), vm(R, Z), vm(4, R, Z),

time: 35.4 us -> 34.8 us (0.983)
  Pallas kernels: 34.6 us -> 34 us
    pallas_call x1, Pallas kernels: 33.4 us -> 32.8 us  [on_device(): pl.pallas_call(functools.partial(kernel, sizes, X, Y, Z), out_shape=(pltp...]
where the time goes in v5:
time: 34.8 us; the launch traced here: 34.7 us
  Pallas kernels  34 us (98%)
  between operations  0.64 us (2%)
    pallas_call x1, Pallas kernels, on_device(): pl.pallas_call(functools.partial(kernel, sizes, X, Y, Z), out_shape=(pltp...  32.8 us
    pallas_call x1, Pallas kernels, on_device(): pl.pallas_call(publish, out_shape=(jax.ShapeDtypeStruct(size_field_modes....  1.23 us

profile of v5, /device:TPU:0, one launch (start us, length us, event | category | flops | bytes accessed | tf_op | source)
XLA Modules:
  0.0 34.7 jit_solution(4507831015727903364)
XLA Ops:
  0.6 32.8 %shard_map.67 = (f32[27,2,2,128]{3,2,1,0:T(2,128)S(1)}, f32[3,6,6,384]{3,2,1,0:T(8,128)S(1)}, f32[1,128]{1,0:T(1,128)S(1)}) custom-call(f32[3,6,6,384]{3,2,1,0:T(8,128)} %disp_in.1, f32[27,2,2,128]{3,2,1,0:T(2,128)} %modes_in.1, f32[3,2,2,128]{3,2,1,0:T(2,128)} %vel_in.1, f32[37,8,128]{2,1,0:T(8,128)} %constant.2.clone.tab_in), custom_call_target="tpu_custom_call" | custom-call | tf_op jit(solution)/shard_map/pallas_call | solution.py:889
  33.4 1.2 %shard_map.68 = (f32[27,2,2,128]{3,2,1,0:T(2,128)}, f32[3,6,6,384]{3,2,1,0:T(8,128)}, f32[3]{0:T(128)}) custom-call(f32[27,2,2,128]{3,2,1,0:T(2,128)S(1)} %get-tuple-element.6.adv, f32[3,6,6,384]{3,2,1,0:T(8,128)S(1)} %get-tuple-element.7.grad, f32[1,128]{1,0:T(1,128)S(1)} %get-tuple-element.8.checks), custom_call_target="tpu_custom_call" | custom-call | tf_op jit(solution)/shard_map/pallas_call | solution.py:913

commit v6 on v5

--- a/solution.py
+++ b/solution.py
@@ -69,6 +69,7 @@
             col[4 * e : 4 * e + 4] = legendre[:, b]
             blocks.append(col)
     blocks.append(np.tile(weights, Y))
+    blocks += [np.tile(value[:, m], Y) for m in range(4)] + [np.tile(slope[:, m], Y) for m in range(4)]
     stacked = np.stack(blocks).astype(np.float32)
     return np.ascontiguousarray(np.broadcast_to(stacked[:, :, None], stacked.shape + (Z,)))
 
@@ -471,40 +472,49 @@
                 t = jnp.where(lanes < EDGE, left, jnp.where(lanes >= Z - EDGE, right, t))
                 U[m, ix * Y : ix * Y + Y, :] = (1.0 / scale[m]) * t[0:Y]
 
+    def apply(T, x, anti, parts=None):
+        e0, e1, o0, o1 = parts or (x[0] + x[3], x[1] + x[2], x[0] - x[3], x[1] - x[2])
+        out = [None] * 4
+        for p in range(2):
+            a = float(0.5 * (T[p, 0] + T[p, 3])) * e0 + float(0.5 * (T[p, 1] + T[p, 2])) * e1
+            b = float(0.5 * (T[p, 0] - T[p, 3])) * o0 + float(0.5 * (T[p, 1] - T[p, 2])) * o1
+            out[p] = a + b
+            out[3 - p] = b - a if anti else a - b
+        return out
+
+    def halves(x):
+        return x[0] + x[3], x[1] + x[2], x[0] - x[3], x[1] - x[2]
+
+    oM = oW + 1
+    element = row // 4
+
     def yz_of(src):
         def yz(i, carry):
             for c in range(3):
                 yv, yd = [], []
                 for k in range(4):
                     sv = sd = None
-                    for j in range(NY + 1):
-                        x = src[c, i, k, j : j + 1, :]
-                        tv, td = tab[oTV + j] * x, tab[oTD + j] * x
+                    for m in range(4):
+                        x = src[c, i, k, 3 * (Y - 1) + m : 3 * (Y - 1) + m + 1, :]
+                        for e in range(Y - 2, -1, -1):
+                            x = jnp.where(element == e, src[c, i, k, 3 * e + m : 3 * e + m + 1, :], x)
+                        tv, td = tab[oM + m] * x, tab[oM + 4 + m] * x
                         sv = tv if sv is None else sv + tv
                         sd = td if sd is None else sd + td
                     yv.append(sv)
                     yd.append(sd)
-                for r in range(4):
-                    A[0, c, i, r] = sum(float(value[r, k]) * yv[k] for k in range(4))
-                    A[1, c, i, r] = sum(float(value[r, k]) * yd[k] for k in range(4))
-                    A[2, c, i, r] = sum(float(slope[r, k]) * yv[k] for k in range(4))
+                parts = halves(yv)
+                outs = apply(value, yv, False, parts), apply(value, yd, False), apply(slope, yv, True, parts)
+                for d in range(3):
+                    for r in range(4):
+                        A[d, c, i, r] = outs[d][r]
             return carry
 
         lax.fori_loop(0, NX + 1, yz, 0)
 
     def slopes_at(ix, r, c, d):
         tb = slope if d == 0 else value
-        x = [A[d, c, 3 * ix + m, r] for m in range(4)]
-        e0, e1, o0, o1 = x[0] + x[3], x[1] + x[2], x[0] - x[3], x[1] - x[2]
-        even = lambda p, m: float(0.5 * (tb[p, m] + tb[p, 3 - m]))
-        odd = lambda p, m: float(0.5 * (tb[p, m] - tb[p, 3 - m]))
-        out = [None] * 4
-        for p in range(2):
-            a = even(p, 0) * e0 + even(p, 1) * e1
-            b = odd(p, 0) * o0 + odd(p, 1) * o1
-            out[p] = a + b
-            out[3 - p] = b - a if d == 0 else a - b
-        return out
+        return apply(tb, [A[d, c, 3 * ix + m, r] for m in range(4)], d == 0)
 
     def jacobians(t):
         ix, r = t // 4, t % 4
@@ -643,26 +653,20 @@
     esum = lax.fori_loop(0, 4 * X, gauss, zero)
 
     def back_c(c, carry):
+        spread = [[[None] * (NX + 1) for _ in range(4)] for _ in range(3)]
+        for d in range(3):
+            tb = slope if d == 0 else value
+            for r in range(4):
+                for ix in range(X):
+                    out = apply(tb.T, [G[d, c, ix, p, r] for p in range(4)], d == 0)
+                    for m in range(4):
+                        was = spread[d][r][3 * ix + m]
+                        spread[d][r][3 * ix + m] = out[m] if was is None else was + out[m]
         for i in range(NX + 1):
-            bv = [None] * 4
-            bd = [None] * 4
-            for r in range(4):
-                ga = []
-                for d in range(3):
-                    tb = slope if d == 0 else value
-                    acc = None
-                    for ix in range(X):
-                        m = i - 3 * ix
-                        if 0 <= m <= 3:
-                            for p in range(4):
-                                term = float(tb[p, m]) * G[d, c, ix, p, r]
-                                acc = term if acc is None else acc + term
-                    ga.append(acc)
-                for k in range(4):
-                    tv = float(value[r, k]) * ga[0] + float(slope[r, k]) * ga[2]
-                    td = float(value[r, k]) * ga[1]
-                    bv[k] = tv if bv[k] is None else bv[k] + tv
-                    bd[k] = td if bd[k] is None else bd[k] + td
+            ga = [[spread[d][r][i] for r in range(4)] for d in range(3)]
+            first, third = apply(value.T, ga[0], False), apply(slope.T, ga[2], True)
+            bv = [first[k] + third[k] for k in range(4)]
+            bd = apply(value.T, ga[1], False)
             for k in range(4):
                 B[0, i, k] = bv[k]
                 B[1, i, k] = bd[k]

time: 34.8 us -> 34.5 us (level)
  no operation moved by 1% of the time
where the time goes in v6:
time: 34.5 us; the launch traced here: 34.3 us
  Pallas kernels  33.7 us (98%)
  between operations  0.64 us (2%)
    pallas_call x1, Pallas kernels, on_device(): pl.pallas_call(functools.partial(kernel, sizes, X, Y, Z), out_shape=(pltp...  32.5 us
    pallas_call x1, Pallas kernels, on_device(): pl.pallas_call(publish, out_shape=(jax.ShapeDtypeStruct(size_field_modes....  1.23 us

profile of v6, /device:TPU:0, one launch (start us, length us, event | category | flops | bytes accessed | tf_op | source)
XLA Modules:
  0.0 34.3 jit_solution(2863125819515785902)
XLA Ops:
  0.6 32.5 %shard_map.67 = (f32[27,2,2,128]{3,2,1,0:T(2,128)S(1)}, f32[3,6,6,384]{3,2,1,0:T(8,128)S(1)}, f32[1,128]{1,0:T(1,128)S(1)}) custom-call(f32[3,6,6,384]{3,2,1,0:T(8,128)} %disp_in.1, f32[27,2,2,128]{3,2,1,0:T(2,128)} %modes_in.1, f32[3,2,2,128]{3,2,1,0:T(2,128)} %vel_in.1, f32[45,8,128]{2,1,0:T(8,128)} %constant.2.clone.tab_in), custom_call_target="tpu_custom_call" | custom-call | tf_op jit(solution)/shard_map/pallas_call | solution.py:893
  33.1 1.2 %shard_map.68 = (f32[27,2,2,128]{3,2,1,0:T(2,128)}, f32[3,6,6,384]{3,2,1,0:T(8,128)}, f32[3]{0:T(128)}) custom-call(f32[27,2,2,128]{3,2,1,0:T(2,128)S(1)} %get-tuple-element.6.adv, f32[3,6,6,384]{3,2,1,0:T(8,128)S(1)} %get-tuple-element.7.grad, f32[1,128]{1,0:T(1,128)S(1)} %get-tuple-element.8.checks), custom_call_target="tpu_custom_call" | custom-call | tf_op jit(solution)/shard_map/pallas_call | solution.py:917
